TPU v7x, 128 devices: a whole 4x4x4 slice. The times are simulated.
128 devices in a mesh: ia: 16 (over y, x), ja: 8 (over z, core).
Axes of the slice: x: 4, y: 4, z: 4, core: 2. Of those that a mesh axis runs over, the one named last changes fastest.
Arguments:
- slabs: bfloat16 [128, 512, 512], P(('ia', 'ja')), may hold values from -1.1953125 to 1.1953125
- pno_coef: bfloat16 [2048, 256, 128], P(('ia', 'ja')), may hold values from -0.375 to 0.375
- dom_blocks: int32 [2048, 2], P(('ia', 'ja')), may hold values from 0 to 3, as said below
- pair_first: int32 [2048], P(('ia', 'ja')), may hold values from 0 to 7
- pair_second: int32 [2048], P(('ia', 'ja')), may hold values from 0 to 15
- pno_energy: float32 [2048, 128], P(('ia', 'ja')), may hold values from 0.3 to 3
- pair_shift: float32 [2048], P(('ia', 'ja')), may hold values from 0.5 to 2
- margin_i: bfloat16 [2048, 16, 128, 128], P(('ia', 'ja')), may hold values from -0.5 to 0.5
- margin_j: bfloat16 [2048, 16, 128, 128], P(('ia', 'ja')), may hold values from -0.5 to 0.5
- couple_i: float32 [2048, 16], P(('ia', 'ja')), may hold values from -0.45 to 0.45
- couple_j: float32 [2048, 16], P(('ia', 'ja')), may hold values from -0.45 to 0.45
- ask_i: int32 [128, 16, 4], P(('ia', 'ja')), may hold values from 0 to 15, as said below
- ask_j: int32 [128, 8, 4], P(('ia', 'ja')), may hold values from 0 to 15, as said below
- link_i: int32 [2048, 16], P(('ia', 'ja')), may hold values from 0 to 63, as said below
- link_j: int32 [2048, 16], P(('ia', 'ja')), may hold values from 0 to 31, as said below
Outputs:
- amplitudes: float32 [2048, 128, 128], P(('ia', 'ja'))
- density: float32 [512, 512], P(('ia', 'ja'))
Inputs may be any that keep to these rules, and one draw needn't show every extreme that they name: `dom_blocks`: the 2 blocks of a pair are distinct. `ask_i`: for each block g and each peer s, the 4 slots are distinct. `ask_j`: for each block g and each peer s, the 4 slots are distinct. `link_i`: within each aligned block of 16 pairs every value is named at least once. `link_j`: within each aligned block of 16 pairs every value is named at least once.
All inputs are finite; a program needn't handle non-finite values.
Results may differ from a plain program's by a relative error of at most 0.0045.
Values may be sent and summed in bfloat16 or wider, within the bound.
No kernel may reach another device: no remote copies, remote signals or barrier semaphores. Data moves between devices by JAX's collectives and lax.ppermute only.
A program may use at most 128 MiB of HBM per device.

v0:
```python
import functools
import math

import jax
import jax.numpy as jnp
from jax import lax
from jax.experimental import pallas as pl
from jax.experimental.pallas import tpu as pltpu
from jax.sharding import Mesh
from jax.sharding import PartitionSpec as P


BLK = 128
ITERS = 2
IA = ("y", "x")
JA = ("z", "c")
ALL = ("y", "x", "z", "c")
F32 = jnp.float32
BF16 = jnp.bfloat16
GROUP = 4
GROUPS = 4
VMEM_LIMIT = 62 * 1024 * 1024


SMEM = pl.BlockSpec(memory_space=pltpu.SMEM)
WHOLE = pl.BlockSpec(memory_space=pltpu.VMEM)
FAR = pl.BlockSpec(memory_space=pltpu.HBM)


def shifted(value, axis, step):
    return lax.ppermute(value, axis, [(i, (i + step) % 4) for i in range(4)])


def to_peer(value, far, near):
    moves = [
        (z * 2 + c, ((z + far) % 4) * 2 + (c + near) % 2) for z in range(4) for c in range(2)
    ]
    return lax.ppermute(value, JA, moves)


def dot(a, b):
    return jnp.dot(a, b, preferred_element_type=F32)


def dot_t(a, b):
    return lax.dot_general(a, b, (((1,), (1,)), ((), ())), preferred_element_type=F32)


def neighbours(value, axis):
    got = []
    for step in (1, -1, 2):
        got.append(shifted(value, axis, step))
    return got


def ring_of_halves(low, high, axis):
    f_low = shifted(low, axis, 1)
    b_low = shifted(low, axis, -1)
    b_high = shifted(high, axis, -1)
    f_high = shifted(high, axis, 1)
    return [low, high, f_low, f_high, b_low, b_high], f_low, b_high


def across(lines):
    got = []
    for value in lines:
        got.append(lax.ppermute(value, "c", [(0, 1), (1, 0)]))
    return got


def with_asks(rows, ask):
    tile = jnp.zeros((16, rows.shape[1]), BF16)
    tile = lax.dynamic_update_slice(tile, ask.astype(BF16), (0, 0))
    return jnp.concatenate([rows, tile], axis=0)


def ring_place(delta):
    return jnp.where(delta == 0, 0, jnp.where(delta == 3, 1, delta + 1))


PLACE_DELTA = (0, 3, 1, 2)


def in_groups(count, one):
    def group(g, carry):
        one([g * GROUP + i for i in range(GROUP)])
        return carry

    lax.fori_loop(0, count // GROUP, group, 0)


def fetch(pieces, code, row, target, sem):
    row = pl.multiple_of(row, 16)
    for j, ref in enumerate(pieces):

        @pl.when(code == j)
        def _(ref=ref):
            pltpu.make_async_copy(ref.at[pl.ds(row, BLK)], target, sem).start()


def arrived(rows, sems, p):
    for k in range(2):
        target = rows.at[p, pl.ds(k * BLK, BLK)]
        pltpu.make_async_copy(target, target, sems.at[p, k]).wait()


def named(tiles, own, owner_of, out):
    pick = lax.broadcasted_iota(jnp.int32, (16, BLK), 0) == own
    for j in range(tiles.shape[0]):
        row = jnp.sum(jnp.where(pick, tiles[j].astype(F32), 0.0), axis=0, keepdims=True)
        out[pl.ds(owner_of(j), 1)] = row.astype(jnp.int32)


def first_kernel(where, first, dom, coef_t, *refs):
    pieces, (out, asked), (rows, sems, tiles, tile_sem) = refs[:8], refs[8:10], refs[10:]
    z, c = where[2], where[3]

    def start(p, carry):
        orb = first[p]
        code = ((orb % 2 - c) & 1) * 4 + ring_place((orb // 2 - z) & 3)
        for k in range(2):
            target = rows.at[p, pl.ds(k * BLK, BLK)]
            fetch(pieces, code, dom[p, k] * BLK, target, sems.at[p, k])
        return carry

    copies = []
    for j in range(8):
        copies.append(
            pltpu.make_async_copy(
                pieces[j].at[pl.ds(4 * BLK, 16), pl.ds(0, BLK)], tiles.at[j], tile_sem.at[j]
            )
        )
        copies[-1].start()
    lax.fori_loop(0, out.shape[0], start, 0)
    for copy in copies:
        copy.wait()

    def owner_of(j):
        return ((z + PLACE_DELTA[j % 4]) & 3) * 2 + ((c + j // 4) & 1)

    named(tiles, z * 2 + c, owner_of, asked)

    def one(group):
        for p in group:
            arrived(rows, sems, p)
        for p in group:
            out[p] = dot(coef_t[p], rows[p]).astype(BF16)

    in_groups(out.shape[0], one)


def pack(sent, where, asked_i, asked_j, send_i, send_j):
    def rows(peer, carry):
        for r in range(4):
            send_i[peer * 4 + r] = sent[asked_i[peer, r]]
        return carry

    lax.fori_loop(0, 16, rows, 0)
    for d, ref in enumerate(send_j):
        peer = ((where[2] + d // 2) & 3) * 2 + ((where[3] + d % 2) & 1)
        for r in range(4):
            ref[r] = sent[asked_j[peer, r]]


def exchange_kernel(where, second, dom, asked_j, coef_t, projected, scale, *refs):
    pieces, (exch, asked, send_i), send_j = refs[:16], refs[16:19], refs[19:27]
    rows, sems, tiles, tile_sem, sent, asked_i, asked_sem = refs[27:]
    y, x = where[0], where[1]
    units = (2 * BLK + 16, 2 * BLK)

    def start(p, carry):
        orb = second[p]
        place_y = ring_place((orb // 4 - y) & 3)
        place_x = ring_place((orb % 4 - x) & 3)
        for k in range(2):
            block = dom[p, k]
            colour = block // 2
            outer = jnp.where(colour == 0, place_y, place_x)
            inner = jnp.where(colour == 0, place_x, place_y)
            code = colour * 8 + outer * 2 + inner // 2
            row = inner % 2 * jnp.where(colour == 0, units[0], units[1])
            row = row + block % 2 * BLK
            fetch(pieces, code, row, rows.at[p, pl.ds(k * BLK, BLK)], sems.at[p, k])
        return carry

    copies = []
    for j in range(16):
        row = j % 2 * units[0] + 2 * BLK
        copies.append(
            pltpu.make_async_copy(
                pieces[j // 2].at[pl.ds(row, 16), pl.ds(0, BLK)], tiles.at[j], tile_sem.at[j]
            )
        )
        copies[-1].start()
    lax.fori_loop(0, exch.shape[0], start, 0)
    for copy in copies:
        copy.wait()

    def owner_of(j):
        return ((y + PLACE_DELTA[j // 4]) & 3) * 4 + ((x + PLACE_DELTA[j % 4]) & 3)

    named(tiles, y * 4 + x, owner_of, asked)
    to_scalars = pltpu.make_async_copy(asked, asked_i, asked_sem)
    to_scalars.start()

    def one(group):
        for p in group:
            arrived(rows, sems, p)
        other = [dot(coef_t[p], rows[p]).astype(BF16) for p in group]
        for p, right in zip(group, other):
            value = dot_t(projected[p], right)
            exch[p] = value
            sent[p] = (value * scale[p]).astype(BF16)

    in_groups(exch.shape[0], one)
    to_scalars.wait()
    pack(sent, where, asked_i, asked_j, send_i, send_j)


def lefts(p, margin, table, entry, couple):
    lane = lax.broadcasted_iota(jnp.int32, (1, 2 * BLK), 1)
    zero = jnp.zeros((BLK, BLK), BF16)
    result = []
    for n in range(0, 16, 2):
        both = jnp.concatenate([margin[p, n], margin[p, n + 1]], axis=1)
        near = jnp.concatenate(
            [
                jnp.concatenate([table[entry(p, n)], zero], axis=1),
                jnp.concatenate([zero, table[entry(p, n + 1)]], axis=1),
            ],
            axis=0,
        )
        weight = jnp.where(lane < BLK, couple[p, n], couple[p, n + 1])
        result.append((dot(both, near) * weight).astype(BF16))
    return result


def rights(p, margin, left):
    total = jnp.zeros((BLK, BLK), F32)
    for n in range(0, 16, 2):
        both = jnp.concatenate([margin[p, n], margin[p, n + 1]], axis=1)
        total = total + dot_t(left[n // 2], both)
    return total


def couplings(group, margin, table, entry, couple):
    totals, last = [], None
    for p in group:
        left = lefts(p, margin, table, entry, couple)
        if last is not None:
            totals.append(rights(*last))
        last = p, margin, left
    return totals + [rights(*last)]


class Loads:
    def __init__(self, tables, arrays, sem):
        self.tables, self.arrays, self.sem = tables, arrays, sem
        for copy in self.whole():
            copy.start()
        for g in range(GROUPS):
            for copy in self.group(g):
                copy.start()

    def whole(self):
        return [
            pltpu.make_async_copy(source, target, self.sem.at[i])
            for i, (source, target) in enumerate(self.tables)
        ]

    def group(self, g):
        at = pl.ds(g * GROUP, GROUP)
        base = len(self.tables)
        return [
            pltpu.make_async_copy(
                source.at[at], target.at[at], self.sem.at[base + i * GROUPS + g]
            )
            for i, (source, target) in enumerate(self.arrays)
        ]

    def each_group(self, step):
        for copy in self.whole():
            copy.wait()

        def group(g, carry):
            for copy in self.group(g):
                copy.wait()
            step([g * GROUP + i for i in range(GROUP)])
            return carry

        lax.fori_loop(0, GROUPS, group, 0)


def second_kind_kernel(where, link, couple, margin_far, exch_far, *refs):
    parts, out, margin, exch, table, sem = refs[:8], *refs[8:]
    tables = [(ref, table.at[pl.ds(d * 4, 4)]) for d, ref in enumerate(parts)]
    loads = Loads(tables, [(margin_far, margin), (exch_far, exch)], sem)

    def entry(p, n):
        value = link[p, n]
        s = value // 4
        d = ((s // 2 - where[2]) & 3) * 2 + ((s % 2 - where[3]) & 1)
        return d * 4 + value % 4

    def step(group):
        for p, total in zip(group, couplings(group, margin, table, entry, couple)):
            out[p] = exch[p] + total

    loads.each_group(step)


def first_kind(loaded, link, couple):
    margin_far, table_far, base_far, scale_far, margin, table, base, scale, sem = loaded
    arrays = [(margin_far, margin), (base_far, base), (scale_far, scale)]
    loads = Loads([(table_far, table)], arrays, sem)

    def values(group):
        totals = couplings(group, margin, table, lambda p, n: link[p, n], couple)
        return [(p, (base[p] + total) * scale[p]) for p, total in zip(group, totals)]

    return loads, values


def middle_kernel(where, link, couple, asked_i, asked_j, *refs):
    far, send_i, send_j, sent = refs[:4], refs[4], refs[5:13], refs[13]
    loads, values = first_kind(far + refs[14:], link, couple)

    def step(group):
        for p, value in values(group):
            sent[p] = value.astype(BF16)

    loads.each_group(step)
    pack(sent, where, asked_i, asked_j, send_i, send_j)


def last_kernel(factor, link, couple, dom, coef, *refs):
    far, (amp, dens, acc) = refs[:4], refs[4:7]
    loads, values = first_kind(far + refs[7:], link, couple)
    acc[...] = jnp.zeros_like(acc)

    def step(group):
        sent = []
        for p, value in values(group):
            amp[p] = value
            sent.append((p, value.astype(BF16)))
        square = [(p, (dot_t(v, v) + dot(v.T, v)).astype(BF16)) for p, v in sent]
        mapped = [(p, dot(coef[p], v).astype(BF16)) for p, v in square]
        blocks = [(p, dot_t(v, coef[p])) for p, v in mapped]
        for p, block in blocks:
            for k in range(2):
                for m in range(2):
                    at = dom[p, k], dom[p, m]
                    acc[at] = acc[at] + block[k * BLK : (k + 1) * BLK, m * BLK : (m + 1) * BLK]

    loads.each_group(step)
    for k in range(4):
        for m in range(4):
            dens[k * BLK : (k + 1) * BLK, m * BLK : (m + 1) * BLK] = (acc[k, m] * factor).astype(
                BF16
            )


def params():
    return pltpu.CompilerParams(vmem_limit_bytes=VMEM_LIMIT)


def cost(flops, size):
    return pl.CostEstimate(flops=flops, bytes_accessed=size, transcendentals=0)


def steps(
    slabs,
    pno_coef,
    dom_blocks,
    pair_first,
    pair_second,
    pno_energy,
    pair_shift,
    margin_i,
    margin_j,
    couple_i,
    couple_j,
    ask_i,
    ask_j,
    link_i,
    link_j,
):
    pairs, domain, pno = pno_coef.shape
    pao, aux = slabs.shape[1:]
    where = jnp.stack([lax.axis_index(a) for a in ALL]).astype(jnp.int32)
    slab = slabs.reshape(pao, aux)
    top = with_asks(slab[: pao // 2], ask_i.reshape(ask_i.shape[1:]))
    bottom = slab[pao // 2 :]
    line = with_asks(slab, ask_j.reshape(ask_j.shape[1:]))
    near_x = neighbours(top, "x")
    near_y = neighbours(bottom, "y")
    lines = [line] + neighbours(line, "z")
    by_x, relay_x, back_x = ring_of_halves(
        jnp.concatenate([top, near_x[0]], axis=0), jnp.concatenate(near_x[1:], axis=0), "y"
    )
    by_y, relay_y, back_y = ring_of_halves(
        jnp.concatenate([bottom, near_y[0]], axis=0), jnp.concatenate(near_y[1:], axis=0), "x"
    )
    lines += across(lines)
    by_x += [shifted(relay_x, "y", 1), shifted(back_x, "y", -1)]
    by_y += [shifted(relay_y, "x", 1), shifted(back_y, "x", -1)]
    pieces = by_x + by_y
    scale = -1.0 / (pno_energy[:, :, None] + pno_energy[:, None, :] + pair_shift[:, None, None])
    coef_t = pno_coef.swapaxes(1, 2)

    block = jax.ShapeDtypeStruct((pairs, pno, pno), F32)
    send_types = [jax.ShapeDtypeStruct((64, pno, pno), BF16)] + [
        jax.ShapeDtypeStruct((4, pno, pno), BF16)
    ] * 8
    fetched = [pltpu.VMEM((pairs, domain, aux), BF16), pltpu.SemaphoreType.DMA((pairs, 2))]
    projected, asked_j = pl.pallas_call(
        first_kernel,
        out_shape=[
            jax.ShapeDtypeStruct((pairs, pno, aux), BF16),
            jax.ShapeDtypeStruct((8, BLK), jnp.int32),
        ],
        in_specs=[SMEM] * 3 + [WHOLE] + [FAR] * 8,
        out_specs=[WHOLE] * 2,
        scratch_shapes=fetched
        + [pltpu.VMEM((8, 16, BLK), BF16), pltpu.SemaphoreType.DMA((8,))],
        compiler_params=params(),
        cost_estimate=cost(pairs * pno * domain * aux * 2, 6 << 20),
        name="project_first",
    )(where, pair_first, dom_blocks, coef_t, *lines)

    exch, asked_i, *sends = pl.pallas_call(
        exchange_kernel,
        out_shape=[block, jax.ShapeDtypeStruct((16, BLK), jnp.int32)] + send_types,
        in_specs=[SMEM] * 4 + [WHOLE] * 3 + [FAR] * 16,
        out_specs=[WHOLE] * 11,
        scratch_shapes=fetched
        + [
            pltpu.VMEM((16, 16, BLK), BF16),
            pltpu.SemaphoreType.DMA((16,)),
            pltpu.VMEM((pairs, pno, pno), BF16),
            pltpu.SMEM((16, BLK), jnp.int32),
            pltpu.SemaphoreType.DMA,
        ],
        compiler_params=params(),
        cost_estimate=cost(pairs * pno * domain * aux * 3, 10 << 20),
        name="exchange",
    )(where, pair_second, dom_blocks, asked_j, coef_t, projected, scale, *pieces)

    work = 16 * pairs * pno**3 * 4
    margin = pltpu.VMEM((pairs, 16, pno, pno), BF16)
    values = pltpu.VMEM((pairs, pno, pno), F32)
    first_scratch = [
        margin,
        pltpu.VMEM((64, pno, pno), BF16),
        values,
        values,
        pltpu.SemaphoreType.DMA((1 + 3 * GROUPS,)),
    ]
    for iteration in range(ITERS):
        send_i, send_j = sends[0], sends[1:]
        table_i = lax.all_to_all(
            send_i.reshape(16, 4, pno, pno), IA, split_axis=0, concat_axis=0, tiled=True
        ).reshape(64, pno, pno)
        parts = {0: send_j[0]}
        for d in (6, 2, 7, 3, 4, 5, 1):
            back = ((-(d // 2)) % 4) * 2 + d % 2
            parts[d] = to_peer(send_j[back], back // 2, back % 2)
        base = pl.pallas_call(
            second_kind_kernel,
            out_shape=block,
            in_specs=[SMEM] * 3 + [FAR] * 10,
            out_specs=WHOLE,
            scratch_shapes=[
                margin,
                values,
                pltpu.VMEM((32, pno, pno), BF16),
                pltpu.SemaphoreType.DMA((8 + 2 * GROUPS,)),
            ],
            compiler_params=params(),
            cost_estimate=cost(work, 12 << 20),
            name="couple_second",
        )(where, link_j, couple_j, margin_j, exch, *(parts[d] for d in range(8)))
        large = (margin_i, table_i, base, scale)
        if iteration < ITERS - 1:
            sends = pl.pallas_call(
                middle_kernel,
                out_shape=send_types,
                in_specs=[SMEM] * 5 + [FAR] * 4,
                out_specs=[WHOLE] * 9,
                scratch_shapes=[pltpu.VMEM((pairs, pno, pno), BF16)] + first_scratch,
                compiler_params=params(),
                cost_estimate=cost(work, 14 << 20),
                name="couple_first",
            )(where, link_i, couple_i, asked_i, asked_j, *large)
        else:
            factor = 1.0 / math.sqrt(pairs * lax.axis_size(ALL))
            amplitudes, partial_sum = pl.pallas_call(
                functools.partial(last_kernel, factor),
                out_shape=[block, jax.ShapeDtypeStruct((pao, pao), BF16)],
                in_specs=[SMEM] * 3 + [WHOLE] + [FAR] * 4,
                out_specs=[WHOLE] * 2,
                scratch_shapes=[pltpu.VMEM((4, 4, BLK, BLK), F32)] + first_scratch,
                compiler_params=params(),
                cost_estimate=cost(work, 16 << 20),
                name="couple_last",
            )(link_i, couple_i, dom_blocks, pno_coef, *large)
    split = partial_sum.reshape(-1, 4, pao)
    got = lax.all_to_all(split, ALL, split_axis=0, concat_axis=0, tiled=True)
    return amplitudes, jnp.sum(got.astype(F32), axis=0)


def solution(mesh):
    split = Mesh(mesh.devices.reshape(4, 4, 4, 2), ALL)
    ranks = (3, 3, 2, 1, 1, 2, 1, 4, 4, 2, 2, 3, 3, 2, 2)
    placed = tuple(P(ALL, *(None,) * (rank - 1)) for rank in ranks)
    return jax.shard_map(
        steps,
        mesh=split,
        in_specs=placed,
        out_specs=(P(ALL, None, None), P(ALL, None)),
        check_vma=False,
    )
```

profile of v0, /device:TPU:0, one launch (start us, length us, event | category | flops | bytes accessed | tf_op | source)
XLA Modules:
  0.0 223.0 jit_solution(11133887494468838125)
XLA Ops:
  0.6 1.1 slice_bitcast_fusion
  3.3 2.9 %collective-permute-start.8 = (bf16[272,512]{1,0:T(8,128)(2,1)}, bf16[272,512]{1,0:T(8,128)(2,1)}, u32[]{:S(2)}, u32[]{:S(2)}) collective-permute-start(bf16[272,512]{1,0:T(8,128)(2,1)} %pad_maximum_fusion.2), channel_id=1, source_target_pairs={{0,24},{8,0},{16,8},{24,16},{1,25},{9,1},{17,9},{25,17},{2,26},{10... | collective-permute-start | bytes 835592 | tf_op jit(solution)/shard_map/ppermute | solution.py:31
  7.0 3.0 %collective-permute-start.17 = (bf16[256,512]{1,0:T(8,128)(2,1)S(1)}, bf16[256,512]{1,0:T(8,128)(2,1)S(1)}, u32[]{:S(2)}, u32[]{:S(2)}) collective-permute-start(bf16[256,512]{1,0:T(8,128)(2,1)S(1)} %get-tuple-element.50), channel_id=1, source_target_pairs={{0,96},{32,0},{64,32},{96,64},{1,97},{33,1},{65,33},{97,65},{2,98}... | collective-permute-start | bytes 786440 | tf_op jit(solution)/shard_map/ppermute | solution.py:31
  11.7 8.9 %collective-permute-done.17 = bf16[256,512]{1,0:T(8,128)(2,1)S(1)} collective-permute-done((bf16[256,512]{1,0:T(8,128)(2,1)S(1)}, bf16[256,512]{1,0:T(8,128)(2,1)S(1)}, u32[]{:S(2)}, u32[]{:S(2)}) %collective-permute-start.17) | collective-permute-done | bytes 262176 | tf_op jit(solution)/shard_map/ppermute | solution.py:31
  20.6 1.9 collective-permute-start
  22.5 2.2 collective-permute-start.1
  24.7 3.5 %collective-permute-start.2 = (bf16[528,512]{1,0:T(8,128)(2,1)S(1)}, bf16[528,512]{1,0:T(8,128)(2,1)S(1)}, u32[]{:S(2)}, u32[]{:S(2)}) collective-permute-start(bf16[528,512]{1,0:T(8,128)(2,1)S(1)} %fusion.1.refs_0_), channel_id=1, source_target_pairs={{0,4},{2,6},{4,0},{6,2},{1,5},{3,7},{5,1},{7,3},{8,12},{10,14},{12... | collective-permute-start | bytes 1622024 | tf_op jit(solution)/shard_map/ppermute | solution.py:31
  29.3 1.3 constant_dynamic-update-slice_fusion.1
  30.6 8.2 %collective-permute-done.7 = bf16[272,512]{1,0:T(8,128)(2,1)S(1)} collective-permute-done((bf16[272,512]{1,0:T(8,128)(2,1)}, bf16[272,512]{1,0:T(8,128)(2,1)S(1)}, u32[]{:S(2)}, u32[]{:S(2)}) %collective-permute-start.7) | collective-permute-done | bytes 278560 | tf_op jit(solution)/shard_map/ppermute | solution.py:31
  39.1 1.7 collective-permute-start.19
  40.9 3.4 %collective-permute-done.1.refs_2_ = bf16[528,512]{1,0:T(8,128)(2,1)S(1)} collective-permute-done((bf16[528,512]{1,0:T(8,128)(2,1)S(1)}, bf16[528,512]{1,0:T(8,128)(2,1)S(1)}, u32[]{:S(2)}, u32[]{:S(2)}) %collective-permute-start.1) | collective-permute-done | bytes 540704 | tf_op jit(solution)/shard_map/ppermute | solution.py:31
  44.2 4.3 %collective-permute-start.13 = (bf16[544,512]{1,0:T(8,128)(2,1)S(1)}, bf16[544,512]{1,0:T(8,128)(2,1)}, u32[]{:S(2)}, u32[]{:S(2)}) collective-permute-start(bf16[544,512]{1,0:T(8,128)(2,1)S(1)} %constant_dynamic-update-slice_fusion.refs_1_), channel_id=1, source_target_pairs={{0,96},{32,0},{64,32},{96,64},{1,97},{33,1},{65,33},{97,65},{2,98}... | collective-permute-start | bytes 1671176 | tf_op jit(solution)/shard_map/ppermute | solution.py:31
  50.2 2.4 %collective-permute-start.21 = (bf16[512,512]{1,0:T(8,128)(2,1)S(1)}, bf16[512,512]{1,0:T(8,128)(2,1)S(1)}, u32[]{:S(2)}, u32[]{:S(2)}) collective-permute-start(bf16[512,512]{1,0:T(8,128)(2,1)S(1)} %pad_maximum_fusion.1.refs_8_), channel_id=1, source_target_pairs={{0,24},{8,0},{16,8},{24,16},{1,25},{9,1},{17,9},{25,17},{2,26},{10... | collective-permute-start | bytes 1572872 | tf_op jit(solution)/shard_map/ppermute | solution.py:31
  52.7 1.0 collective-permute-done.22.refs_13_
  53.7 1.6 collective-permute-done.19.refs_10_
  55.3 9.8 %collective-permute-done.20.refs_11_ = bf16[512,512]{1,0:T(8,128)(2,1)S(1)} collective-permute-done((bf16[512,512]{1,0:T(8,128)(2,1)S(1)}, bf16[512,512]{1,0:T(8,128)(2,1)S(1)}, u32[]{:S(2)}, u32[]{:S(2)}) %collective-permute-start.20) | collective-permute-done | bytes 524320 | tf_op jit(solution)/shard_map/ppermute | solution.py:31
  65.7 4.7 %collective-permute-done.11.refs_3_ = bf16[544,512]{1,0:T(8,128)(2,1)S(1)} collective-permute-done((bf16[544,512]{1,0:T(8,128)(2,1)S(1)}, bf16[544,512]{1,0:T(8,128)(2,1)S(1)}, u32[]{:S(2)}, u32[]{:S(2)}) %collective-permute-start.11) | collective-permute-done | bytes 557088 | tf_op jit(solution)/shard_map/ppermute | solution.py:31
  71.2 7.7 %collective-permute-done.10.refs_2_ = bf16[544,512]{1,0:T(8,128)(2,1)} collective-permute-done((bf16[544,512]{1,0:T(8,128)(2,1)S(1)}, bf16[544,512]{1,0:T(8,128)(2,1)}, u32[]{:S(2)}, u32[]{:S(2)}) %collective-permute-start.10) | collective-permute-done | bytes 557088 | tf_op jit(solution)/shard_map/ppermute | solution.py:31
  79.0 1.2 collective-permute-start.15
  81.1 2.2 collective-permute-start.24
  84.8 1.3 copy.17
  86.7 1.4 add_divide_fusion.scale.refs_3_
  88.1 5.7 %project_first.1 = (bf16[16,128,512]{2,1,0:T(8,128)(2,1)}, s32[8,128]{1,0:T(8,128)}) custom-call(s32[4]{0:T(128)} %pad_add_fusion.where, s32[16]{0:T(128)} %first.1, s32[16,2]{1,0:T(8,128)} %copy.22.dom, bf16[16,128,256]{2,1,0:T(8,128)(2,1)} %bitcast.18, bf16[528,512]{1,0:T(8,128)(2,1)} %copy-done.2, bf16[528,512]{1,0:T(8,128)(2,1)} %copy-done.9, ...), custom_call_target="tpu_custom_call" | custom-call | flops 536870912 | bytes 6291456 | tf_op jit(solution)/shard_map/project_first/pallas_call | solution.py:416
  93.9 1.2 collective-permute-done.23.refs_14_
  95.0 8.4 %exchange.1 = (f32[16,128,128]{2,1,0:T(8,128)}, s32[16,128]{1,0:T(8,128)}, bf16[64,128,128]{2,1,0:T(8,128)(2,1)}, bf16[4,128,128]{2,1,0:T(8,128)(2,1)}, bf16[4,1...) custom-call(s32[4]{0:T(128)} %pad_add_fusion.where, ...), custom_call_target="tpu_custom_call" | custom-call | flops 805306368 | bytes 10485760 | tf_op jit(solution)/shard_map/exchange/pallas_call | solution.py:431
  103.6 5.2 %all-to-all-start = ((bf16[16,4,128,128]{3,2,1,0:T(8,128)(2,1)}), bf16[16,4,128,128]{3,2,1,0:T(8,128)(2,1)}, u32[]{:S(2)}, u32[]{:S(2)}) async-start(bf16[16,4,128,128]{3,2,1,0:T(8,128)(2,1)} %bitcast.20), calls=%async_computation | async-start | bytes 4194304 | tf_op jit(solution)/shard_map/all_to_all | solution.py:461
  110.7 2.1 collective-permute-start.28
  112.9 1.3 collective-permute-start.29
  116.9 1.7 collective-permute-done.28.refs_4_
  118.6 2.0 collective-permute-done.29.refs_5_
  120.7 3.2 %collective-permute-done.30.refs_6_ = bf16[4,128,128]{2,1,0:T(8,128)(2,1)S(1)} collective-permute-done((bf16[4,128,128]{2,1,0:T(8,128)(2,1)S(1)}, bf16[4,128,128]{2,1,0:T(8,128)(2,1)S(1)}, u32[]{:S(2)}, u32[]{:S(2)}) %collective-permute-start.30) | collective-permute-done | bytes 131104 | tf_op jit(solution)/shard_map/ppermute | solution.py:38
  123.9 2.7 %collective-permute-done.31.refs_7_ = bf16[4,128,128]{2,1,0:T(8,128)(2,1)S(1)} collective-permute-done((bf16[4,128,128]{2,1,0:T(8,128)(2,1)S(1)}, bf16[4,128,128]{2,1,0:T(8,128)(2,1)S(1)}, u32[]{:S(2)}, u32[]{:S(2)}) %collective-permute-start.31) | collective-permute-done | bytes 131104 | tf_op jit(solution)/shard_map/ppermute | solution.py:38
  127.2 10.7 %couple_second.2.refs_2_ = f32[16,128,128]{2,1,0:T(8,128)} custom-call(s32[4]{0:T(128)} %pad_add_fusion.where, s32[16,16]{1,0:T(8,128)} %link.6, f32[16,16]{1,0:T(8,128)} %couple.6, bf16[16,16,128,128]{3,2,1,0:T(8,128)(2,1)} %margin_far.3, f32[16,128,128]{2,1,0:T(8,128)} %get-tuple-element.30.exch_far, bf16[4,128,128]{2,1,0:T(8,128)(2,1)} %get-tuple-element.31.refs_0_, ...), custom_call_target="tpu_custom_call" | custom-call | flops 2147483648 | bytes 12582912 | tf_op jit(solution)/shard_map/couple_second/pallas_call | solution.py:468
  137.9 10.8 %couple_first.1 = (bf16[64,128,128]{2,1,0:T(8,128)(2,1)}, bf16[4,128,128]{2,1,0:T(8,128)(2,1)}, bf16[4,128,128]{2,1,0:T(8,128)(2,1)}, bf16[4,128,128]{2,1,0:T(8,...) custom-call(s32[4]{0:T(128)} %pad_add_fusion.where, ...), custom_call_target="tpu_custom_call" | custom-call | flops 2147483648 | bytes 14680064 | tf_op jit(solution)/shard_map/couple_first/pallas_call | solution.py:485
  148.8 7.4 %all-to-all-start.1 = ((bf16[16,4,128,128]{3,2,1,0:T(8,128)(2,1)}), bf16[16,4,128,128]{3,2,1,0:T(8,128)(2,1)}, u32[]{:S(2)}, u32[]{:S(2)}) async-start(bf16[16,4,128,128]{3,2,1,0:T(8,128)(2,1)} %bitcast.21), calls=%async_computation.1 | async-start | bytes 4194304 | tf_op jit(solution)/shard_map/all_to_all | solution.py:461
  156.8 1.9 collective-permute-start.34
  158.8 1.4 collective-permute-start.35
  160.2 1.8 collective-permute-start.36
  163.2 1.2 collective-permute-done.34.refs_3_
  164.4 2.3 %collective-permute-done.35.refs_4_ = bf16[4,128,128]{2,1,0:T(8,128)(2,1)S(1)} collective-permute-done((bf16[4,128,128]{2,1,0:T(8,128)(2,1)S(1)}, bf16[4,128,128]{2,1,0:T(8,128)(2,1)S(1)}, u32[]{:S(2)}, u32[]{:S(2)}) %collective-permute-start.35) | collective-permute-done | bytes 131104 | tf_op jit(solution)/shard_map/ppermute | solution.py:38
  166.7 1.7 collective-permute-done.36.refs_5_
  168.3 3.4 %collective-permute-done.37.refs_6_ = bf16[4,128,128]{2,1,0:T(8,128)(2,1)S(1)} collective-permute-done((bf16[4,128,128]{2,1,0:T(8,128)(2,1)S(1)}, bf16[4,128,128]{2,1,0:T(8,128)(2,1)S(1)}, u32[]{:S(2)}, u32[]{:S(2)}) %collective-permute-start.37) | collective-permute-done | bytes 131104 | tf_op jit(solution)/shard_map/ppermute | solution.py:38
  171.7 2.7 %collective-permute-done.38.refs_7_ = bf16[4,128,128]{2,1,0:T(8,128)(2,1)S(1)} collective-permute-done((bf16[4,128,128]{2,1,0:T(8,128)(2,1)S(1)}, bf16[4,128,128]{2,1,0:T(8,128)(2,1)S(1)}, u32[]{:S(2)}, u32[]{:S(2)}) %collective-permute-start.38) | collective-permute-done | bytes 131104 | tf_op jit(solution)/shard_map/ppermute | solution.py:38
  175.1 10.8 %couple_second.3.refs_2_ = f32[16,128,128]{2,1,0:T(8,128)} custom-call(s32[4]{0:T(128)} %pad_add_fusion.where, s32[16,16]{1,0:T(8,128)} %link.6, f32[16,16]{1,0:T(8,128)} %couple.6, bf16[16,16,128,128]{3,2,1,0:T(8,128)(2,1)} %margin_far.3, f32[16,128,128]{2,1,0:T(8,128)} %get-tuple-element.30.exch_far, bf16[4,128,128]{2,1,0:T(8,128)(2,1)} %get-tuple-element.40.refs_0_, ...), custom_call_target="tpu_custom_call" | custom-call | flops 2147483648 | bytes 12582912 | tf_op jit(solution)/shard_map/couple_second/pallas_call | solution.py:468
  185.9 3.2 %all-to-all-done.1 = bf16[16,4,128,128]{3,2,1,0:T(8,128)(2,1)} async-done(((bf16[16,4,128,128]{3,2,1,0:T(8,128)(2,1)}), bf16[16,4,128,128]{3,2,1,0:T(8,128)(2,1)}, u32[]{:S(2)}, u32[]{:S(2)}) %all-to-all-start.1) | async-done | bytes 2097184 | tf_op jit(solution)/shard_map/all_to_all | solution.py:461
  189.1 12.1 %couple_last.1 = (f32[16,128,128]{2,1,0:T(8,128)}, bf16[512,512]{1,0:T(8,128)(2,1)}) custom-call(s32[16,16]{1,0:T(8,128)} %link.7, f32[16,16]{1,0:T(8,128)} %couple.7, s32[16,2]{1,0:T(8,128)} %copy.22.dom, bf16[16,256,128]{2,1,0:T(8,128)(2,1)} %coef.1, bf16[16,16,128,128]{3,2,1,0:T(8,128)(2,1)} %refs_0_.3, bf16[64,128,128]{2,1,0:T(8,128)(2,1)} %bitcast.13.refs_1_, ...), custom_call_target="tpu_custom_call" | custom-call | flops 2147483648 | bytes 16777216 | tf_op jit(solution)/shard_map/couple_last/pallas_call | solution.py:497
  201.2 1.2 reshape.36
  202.4 19.7 %all_to_all.15 = bf16[128,4,512]{2,1,0:T(4,128)(2,1)S(1)} all-to-all(bf16[128,4,512]{2,1,0:T(4,128)(2,1)S(1)} %reshape.36), channel_id=1, replica_groups=mesh['y'=4,'x'=4,'z'=4,'c'=2] {'y','x','z','c'}, dimensions={0} | all-to-all | bytes 1048576 | tf_op jit(solution)/shard_map/all_to_all | solution.py:508
  (161 shorter events, 20.5 us)
Async XLA Ops:
  3.3 24.9 %collective-permute-start.8 = (bf16[272,512]{1,0:T(8,128)(2,1)}, bf16[272,512]{1,0:T(8,128)(2,1)}, u32[]{:S(2)}, u32[]{:S(2)}) collective-permute-start(bf16[272,512]{1,0:T(8,128)(2,1)} %pad_maximum_fusion.2), channel_id=1, source_target_pairs={{0,24},{8,0},{16,8},{24,16},{1,25},{9,1},{17,9},{25,17},{2,26},{10... | collective-permute-start | bytes 835592 | tf_op jit(solution)/shard_map/ppermute | solution.py:31
  6.2 22.1 %collective-permute-start.9 = (bf16[272,512]{1,0:T(8,128)(2,1)}, bf16[272,512]{1,0:T(8,128)(2,1)S(1)}, u32[]{:S(2)}, u32[]{:S(2)}) collective-permute-start(bf16[272,512]{1,0:T(8,128)(2,1)} %pad_maximum_fusion.2), channel_id=1, source_target_pairs={{0,16},{8,24},{16,0},{24,8},{1,17},{9,25},{17,1},{25,9},{2,18},{10... | collective-permute-start | bytes 835592 | tf_op jit(solution)/shard_map/ppermute | solution.py:31
  7.0 13.6 %collective-permute-start.17 = (bf16[256,512]{1,0:T(8,128)(2,1)S(1)}, bf16[256,512]{1,0:T(8,128)(2,1)S(1)}, u32[]{:S(2)}, u32[]{:S(2)}) collective-permute-start(bf16[256,512]{1,0:T(8,128)(2,1)S(1)} %get-tuple-element.50), channel_id=1, source_target_pairs={{0,96},{32,0},{64,32},{96,64},{1,97},{33,1},{65,33},{97,65},{2,98}... | collective-permute-start | bytes 786440 | tf_op jit(solution)/shard_map/ppermute | solution.py:31
  10.0 12.5 %collective-permute-start.18 = (bf16[256,512]{1,0:T(8,128)(2,1)S(1)}, bf16[256,512]{1,0:T(8,128)(2,1)S(1)}, u32[]{:S(2)}, u32[]{:S(2)}) collective-permute-start(bf16[256,512]{1,0:T(8,128)(2,1)S(1)} %get-tuple-element.50), channel_id=1, source_target_pairs={{0,64},{32,96},{64,0},{96,32},{1,65},{33,97},{65,1},{97,33},{2,66}... | collective-permute-start | bytes 786440 | tf_op jit(solution)/shard_map/ppermute | solution.py:31
  10.6 14.1 %collective-permute-start.16 = (bf16[256,512]{1,0:T(8,128)(2,1)S(1)}, bf16[256,512]{1,0:T(8,128)(2,1)S(1)}, u32[]{:S(2)}, u32[]{:S(2)}) collective-permute-start(bf16[256,512]{1,0:T(8,128)(2,1)S(1)} %get-tuple-element.50), channel_id=1, source_target_pairs={{0,32},{32,64},{64,96},{96,0},{1,33},{33,65},{65,97},{97,1},{2,34}... | collective-permute-start | bytes 786440 | tf_op jit(solution)/shard_map/ppermute | solution.py:31
  20.6 18.5 %collective-permute-start = (bf16[528,512]{1,0:T(8,128)(2,1)S(1)}, bf16[528,512]{1,0:T(8,128)(2,1)S(1)}, u32[]{:S(2)}, u32[]{:S(2)}) collective-permute-start(bf16[528,512]{1,0:T(8,128)(2,1)S(1)} %fusion.1.refs_0_), channel_id=1, source_target_pairs={{0,2},{2,4},{4,6},{6,0},{1,3},{3,5},{5,7},{7,1},{8,10},{10,12},{12... | collective-permute-start | bytes 1622024 | tf_op jit(solution)/shard_map/ppermute | solution.py:31
  22.5 21.7 %collective-permute-start.1 = (bf16[528,512]{1,0:T(8,128)(2,1)S(1)}, bf16[528,512]{1,0:T(8,128)(2,1)S(1)}, u32[]{:S(2)}, u32[]{:S(2)}) collective-permute-start(bf16[528,512]{1,0:T(8,128)(2,1)S(1)} %fusion.1.refs_0_), channel_id=1, source_target_pairs={{0,6},{2,0},{4,2},{6,4},{1,7},{3,1},{5,3},{7,5},{8,14},{10,8},{12,... | collective-permute-start | bytes 1622024 | tf_op jit(solution)/shard_map/ppermute | solution.py:31
  24.7 23.8 %collective-permute-start.2 = (bf16[528,512]{1,0:T(8,128)(2,1)S(1)}, bf16[528,512]{1,0:T(8,128)(2,1)S(1)}, u32[]{:S(2)}, u32[]{:S(2)}) collective-permute-start(bf16[528,512]{1,0:T(8,128)(2,1)S(1)} %fusion.1.refs_0_), channel_id=1, source_target_pairs={{0,4},{2,6},{4,0},{6,2},{1,5},{3,7},{5,1},{7,3},{8,12},{10,14},{12... | collective-permute-start | bytes 1622024 | tf_op jit(solution)/shard_map/ppermute | solution.py:31
  28.2 21.2 %collective-permute-start.3 = (bf16[528,512]{1,0:T(8,128)(2,1)S(1)}, bf16[528,512]{1,0:T(8,128)(2,1)S(1)}, u32[]{:S(2)}, u32[]{:S(2)}) collective-permute-start(bf16[528,512]{1,0:T(8,128)(2,1)S(1)} %fusion.1.refs_0_), channel_id=1, source_target_pairs={{0,1},{1,0},{2,3},{3,2},{4,5},{5,4},{6,7},{7,6},{8,9},{9,8},{10,11... | collective-permute-start | bytes 1622024 | tf_op jit(solution)/shard_map/ppermute | solution.py:67
  28.2 10.6 %collective-permute-start.7 = (bf16[272,512]{1,0:T(8,128)(2,1)}, bf16[272,512]{1,0:T(8,128)(2,1)S(1)}, u32[]{:S(2)}, u32[]{:S(2)}) collective-permute-start(bf16[272,512]{1,0:T(8,128)(2,1)} %pad_maximum_fusion.2), channel_id=1, source_target_pairs={{0,8},{8,16},{16,24},{24,0},{1,9},{9,17},{17,25},{25,1},{2,10},{10... | collective-permute-start | bytes 835592 | tf_op jit(solution)/shard_map/ppermute | solution.py:31
  29.3 54.8 %copy-start.34 = (s32[16,2]{0,1:T(2,128)S(1)}, s32[16,2]{0,1:T(2,128)}, u32[]{:S(2)}) copy-start(s32[16,2]{0,1:T(2,128)} %param.17) | copy-start | bytes 388
  29.3 55.5 %copy-start = (bf16[16,256,128]{2,1,0:T(8,128)(2,1)S(1)}, bf16[16,256,128]{2,1,0:T(8,128)(2,1)}, u32[]{:S(2)}) copy-start(bf16[16,256,128]{2,1,0:T(8,128)(2,1)} %coef.1) | copy-start | bytes 3145732
  38.8 14.9 %collective-permute-start.22 = (bf16[512,512]{1,0:T(8,128)(2,1)S(1)}, bf16[512,512]{1,0:T(8,128)(2,1)}, u32[]{:S(2)}, u32[]{:S(2)}) collective-permute-start(bf16[512,512]{1,0:T(8,128)(2,1)S(1)} %constant_dynamic-update-slice_fusion.2.refs_9_), channel_id=1, source_target_pairs={{0,24},{8,0},{16,8},{24,16},{1,25},{9,1},{17,9},{25,17},{2,26},{10... | collective-permute-start | bytes 1572872 | tf_op jit(solution)/shard_map/ppermute | solution.py:31
  39.1 41.0 %copy-start.9 = (bf16[528,512]{1,0:T(8,128)(2,1)}, bf16[528,512]{1,0:T(8,128)(2,1)S(1)}, u32[]{:S(2)}) copy-start(bf16[528,512]{1,0:T(8,128)(2,1)S(1)} %collective-permute-done.refs_1_) | copy-start | bytes 1622020
  39.1 16.1 %collective-permute-start.19 = (bf16[512,512]{1,0:T(8,128)(2,1)S(1)}, bf16[512,512]{1,0:T(8,128)(2,1)}, u32[]{:S(2)}, u32[]{:S(2)}) collective-permute-start(bf16[512,512]{1,0:T(8,128)(2,1)S(1)} %pad_maximum_fusion.1.refs_8_), channel_id=1, source_target_pairs={{0,8},{8,16},{16,24},{24,0},{1,9},{9,17},{17,25},{25,1},{2,10},{10... | collective-permute-start | bytes 1572872 | tf_op jit(solution)/shard_map/ppermute | solution.py:31
  40.8 45.2 %copy-start.5 = (bf16[544,512]{1,0:T(8,128)(2,1)}, bf16[544,512]{1,0:T(8,128)(2,1)S(1)}, u32[]{:S(2)}) copy-start(bf16[544,512]{1,0:T(8,128)(2,1)S(1)} %constant_dynamic-update-slice_fusion.refs_1_) | copy-start | bytes 1671172
  44.2 35.9 %copy-start.10 = (bf16[528,512]{1,0:T(8,128)(2,1)}, bf16[528,512]{1,0:T(8,128)(2,1)S(1)}, u32[]{:S(2)}) copy-start(bf16[528,512]{1,0:T(8,128)(2,1)S(1)} %collective-permute-done.1.refs_2_) | copy-start | bytes 1622020
  44.2 21.3 %collective-permute-start.13 = (bf16[544,512]{1,0:T(8,128)(2,1)S(1)}, bf16[544,512]{1,0:T(8,128)(2,1)}, u32[]{:S(2)}, u32[]{:S(2)}) collective-permute-start(bf16[544,512]{1,0:T(8,128)(2,1)S(1)} %constant_dynamic-update-slice_fusion.refs_1_), channel_id=1, source_target_pairs={{0,96},{32,0},{64,32},{96,64},{1,97},{33,1},{65,33},{97,65},{2,98}... | collective-permute-start | bytes 1671176 | tf_op jit(solution)/shard_map/ppermute | solution.py:31
  48.5 16.5 %collective-permute-start.20 = (bf16[512,512]{1,0:T(8,128)(2,1)S(1)}, bf16[512,512]{1,0:T(8,128)(2,1)S(1)}, u32[]{:S(2)}, u32[]{:S(2)}) collective-permute-start(bf16[512,512]{1,0:T(8,128)(2,1)S(1)} %constant_dynamic-update-slice_fusion.2.refs_9_), channel_id=1, source_target_pairs={{0,8},{8,16},{16,24},{24,0},{1,9},{9,17},{17,25},{25,1},{2,10},{10... | collective-permute-start | bytes 1572872 | tf_op jit(solution)/shard_map/ppermute | solution.py:31
  50.2 14.8 %collective-permute-start.21 = (bf16[512,512]{1,0:T(8,128)(2,1)S(1)}, bf16[512,512]{1,0:T(8,128)(2,1)S(1)}, u32[]{:S(2)}, u32[]{:S(2)}) collective-permute-start(bf16[512,512]{1,0:T(8,128)(2,1)S(1)} %pad_maximum_fusion.1.refs_8_), channel_id=1, source_target_pairs={{0,24},{8,0},{16,8},{24,16},{1,25},{9,1},{17,9},{25,17},{2,26},{10... | collective-permute-start | bytes 1572872 | tf_op jit(solution)/shard_map/ppermute | solution.py:31
  52.7 35.4 %copy-start.1 = (bf16[544,512]{1,0:T(8,128)(2,1)}, bf16[544,512]{1,0:T(8,128)(2,1)S(1)}, u32[]{:S(2)}) copy-start(bf16[544,512]{1,0:T(8,128)(2,1)S(1)} %pad_maximum_fusion.refs_0_) | copy-start | bytes 1671172
  52.7 34.1 %copy-start.32 = (f32[16,128]{1,0:T(8,128)S(1)}, f32[16,128]{1,0:T(8,128)}, u32[]{:S(2)}) copy-start(f32[16,128]{1,0:T(8,128)} %param.20) | copy-start | bytes 24580
  53.7 16.7 %collective-permute-start.11 = (bf16[544,512]{1,0:T(8,128)(2,1)S(1)}, bf16[544,512]{1,0:T(8,128)(2,1)S(1)}, u32[]{:S(2)}, u32[]{:S(2)}) collective-permute-start(bf16[544,512]{1,0:T(8,128)(2,1)S(1)} %constant_dynamic-update-slice_fusion.refs_1_), channel_id=1, source_target_pairs={{0,32},{32,64},{64,96},{96,0},{1,33},{33,65},{65,97},{97,1},{2,34}... | collective-permute-start | bytes 1671176 | tf_op jit(solution)/shard_map/ppermute | solution.py:31
  55.3 23.7 %collective-permute-start.10 = (bf16[544,512]{1,0:T(8,128)(2,1)S(1)}, bf16[544,512]{1,0:T(8,128)(2,1)}, u32[]{:S(2)}, u32[]{:S(2)}) collective-permute-start(bf16[544,512]{1,0:T(8,128)(2,1)S(1)} %pad_maximum_fusion.refs_0_), channel_id=1, source_target_pairs={{0,32},{32,64},{64,96},{96,0},{1,33},{33,65},{65,97},{97,1},{2,34}... | collective-permute-start | bytes 1671176 | tf_op jit(solution)/shard_map/ppermute | solution.py:31
  65.1 15.1 %collective-permute-start.4 = (bf16[528,512]{1,0:T(8,128)(2,1)S(1)}, bf16[528,512]{1,0:T(8,128)(2,1)S(1)}, u32[]{:S(2)}, u32[]{:S(2)}) collective-permute-start(bf16[528,512]{1,0:T(8,128)(2,1)S(1)} %collective-permute-done.refs_1_), channel_id=1, source_target_pairs={{0,1},{1,0},{2,3},{3,2},{4,5},{5,4},{6,7},{7,6},{8,9},{9,8},{10,11... | collective-permute-start | bytes 1622024 | tf_op jit(solution)/shard_map/ppermute | solution.py:67
  65.1 16.0 %collective-permute-start.5 = (bf16[528,512]{1,0:T(8,128)(2,1)S(1)}, bf16[528,512]{1,0:T(8,128)(2,1)S(1)}, u32[]{:S(2)}, u32[]{:S(2)}) collective-permute-start(bf16[528,512]{1,0:T(8,128)(2,1)S(1)} %collective-permute-done.1.refs_2_), channel_id=1, source_target_pairs={{0,1},{1,0},{2,3},{3,2},{4,5},{5,4},{6,7},{7,6},{8,9},{9,8},{10,11... | collective-permute-start | bytes 1622024 | tf_op jit(solution)/shard_map/ppermute | solution.py:67
  65.6 17.7 %collective-permute-start.6 = (bf16[528,512]{1,0:T(8,128)(2,1)S(1)}, bf16[528,512]{1,0:T(8,128)(2,1)S(1)}, u32[]{:S(2)}, u32[]{:S(2)}) collective-permute-start(bf16[528,512]{1,0:T(8,128)(2,1)S(1)} %collective-permute-done.2.refs_3_), channel_id=1, source_target_pairs={{0,1},{1,0},{2,3},{3,2},{4,5},{5,4},{6,7},{7,6},{8,9},{9,8},{10,11... | collective-permute-start | bytes 1622024 | tf_op jit(solution)/shard_map/ppermute | solution.py:67
  70.4 23.4 %collective-permute-start.12 = (bf16[544,512]{1,0:T(8,128)(2,1)S(1)}, bf16[544,512]{1,0:T(8,128)(2,1)S(1)}, u32[]{:S(2)}, u32[]{:S(2)}) collective-permute-start(bf16[544,512]{1,0:T(8,128)(2,1)S(1)} %pad_maximum_fusion.refs_0_), channel_id=1, source_target_pairs={{0,96},{32,0},{64,32},{96,64},{1,97},{33,1},{65,33},{97,65},{2,98}... | collective-permute-start | bytes 1671176 | tf_op jit(solution)/shard_map/ppermute | solution.py:31
  79.0 16.1 %collective-permute-start.15 = (bf16[544,512]{1,0:T(8,128)(2,1)}, bf16[544,512]{1,0:T(8,128)(2,1)}, u32[]{:S(2)}, u32[]{:S(2)}) collective-permute-start(bf16[544,512]{1,0:T(8,128)(2,1)} %collective-permute-done.13.refs_5_), channel_id=1, source_target_pairs={{0,96},{32,0},{64,32},{96,64},{1,97},{33,1},{65,33},{97,65},{2,98}... | collective-permute-start | bytes 1671176 | tf_op jit(solution)/shard_map/ppermute | solution.py:31
  80.1 14.9 %collective-permute-start.14 = (bf16[544,512]{1,0:T(8,128)(2,1)}, bf16[544,512]{1,0:T(8,128)(2,1)}, u32[]{:S(2)}, u32[]{:S(2)}) collective-permute-start(bf16[544,512]{1,0:T(8,128)(2,1)} %collective-permute-done.10.refs_2_), channel_id=1, source_target_pairs={{0,32},{32,64},{64,96},{96,0},{1,33},{33,65},{65,97},{97,1},{2,34}... | collective-permute-start | bytes 1671176 | tf_op jit(solution)/shard_map/ppermute | solution.py:31
  81.1 12.8 %collective-permute-start.24 = (bf16[512,512]{1,0:T(8,128)(2,1)}, bf16[512,512]{1,0:T(8,128)(2,1)}, u32[]{:S(2)}, u32[]{:S(2)}) collective-permute-start(bf16[512,512]{1,0:T(8,128)(2,1)} %collective-permute-done.22.refs_13_), channel_id=1, source_target_pairs={{0,24},{8,0},{16,8},{24,16},{1,25},{9,1},{17,9},{25,17},{2,26},{10... | collective-permute-start | bytes 1572872 | tf_op jit(solution)/shard_map/ppermute | solution.py:31
  83.3 11.8 %collective-permute-start.23 = (bf16[512,512]{1,0:T(8,128)(2,1)}, bf16[512,512]{1,0:T(8,128)(2,1)}, u32[]{:S(2)}, u32[]{:S(2)}) collective-permute-start(bf16[512,512]{1,0:T(8,128)(2,1)} %collective-permute-done.19.refs_10_), channel_id=1, source_target_pairs={{0,8},{8,16},{16,24},{24,0},{1,9},{9,17},{17,25},{25,1},{2,10},{10... | collective-permute-start | bytes 1572872 | tf_op jit(solution)/shard_map/ppermute | solution.py:31
  103.6 34.4 %all-to-all-start = ((bf16[16,4,128,128]{3,2,1,0:T(8,128)(2,1)}), bf16[16,4,128,128]{3,2,1,0:T(8,128)(2,1)}, u32[]{:S(2)}, u32[]{:S(2)}) async-start(bf16[16,4,128,128]{3,2,1,0:T(8,128)(2,1)} %bitcast.20), calls=%async_computation | async-start | bytes 4194304 | tf_op jit(solution)/shard_map/all_to_all | solution.py:461
  108.8 5.3 %collective-permute-start.25 = (bf16[4,128,128]{2,1,0:T(8,128)(2,1)S(1)}, bf16[4,128,128]{2,1,0:T(8,128)(2,1)S(1)}, u32[]{:S(2)}, u32[]{:S(2)}) collective-permute-start(bf16[4,128,128]{2,1,0:T(8,128)(2,1)S(1)} %copy-done.46), channel_id=1, source_target_pairs={{0,1},{1,0},{2,3},{3,2},{4,5},{5,4},{6,7},{7,6},{8,9},{9,8},{10,11... | collective-permute-start | bytes 393224 | tf_op jit(solution)/shard_map/ppermute | solution.py:38
  108.9 6.6 %collective-permute-start.26 = (bf16[4,128,128]{2,1,0:T(8,128)(2,1)S(1)}, bf16[4,128,128]{2,1,0:T(8,128)(2,1)S(1)}, u32[]{:S(2)}, u32[]{:S(2)}) collective-permute-start(bf16[4,128,128]{2,1,0:T(8,128)(2,1)S(1)} %copy-done.42), channel_id=1, source_target_pairs={{0,6},{1,7},{2,0},{3,1},{4,2},{5,3},{6,4},{7,5},{8,14},{9,15},{10,... | collective-permute-start | bytes 393224 | tf_op jit(solution)/shard_map/ppermute | solution.py:38
  109.8 7.1 %collective-permute-start.27 = (bf16[4,128,128]{2,1,0:T(8,128)(2,1)S(1)}, bf16[4,128,128]{2,1,0:T(8,128)(2,1)S(1)}, u32[]{:S(2)}, u32[]{:S(2)}) collective-permute-start(bf16[4,128,128]{2,1,0:T(8,128)(2,1)S(1)} %copy-done.40), channel_id=1, source_target_pairs={{0,7},{1,6},{2,1},{3,0},{4,3},{5,2},{6,5},{7,4},{8,15},{9,14},{10,... | collective-permute-start | bytes 393224 | tf_op jit(solution)/shard_map/ppermute | solution.py:38
  110.7 7.9 %collective-permute-start.28 = (bf16[4,128,128]{2,1,0:T(8,128)(2,1)S(1)}, bf16[4,128,128]{2,1,0:T(8,128)(2,1)S(1)}, u32[]{:S(2)}, u32[]{:S(2)}) collective-permute-start(bf16[4,128,128]{2,1,0:T(8,128)(2,1)S(1)} %copy-done.39), channel_id=1, source_target_pairs={{0,4},{1,5},{2,6},{3,7},{4,0},{5,1},{6,2},{7,3},{8,12},{9,13},{10,... | collective-permute-start | bytes 393224 | tf_op jit(solution)/shard_map/ppermute | solution.py:38
  112.9 7.8 %collective-permute-start.29 = (bf16[4,128,128]{2,1,0:T(8,128)(2,1)S(1)}, bf16[4,128,128]{2,1,0:T(8,128)(2,1)S(1)}, u32[]{:S(2)}, u32[]{:S(2)}) collective-permute-start(bf16[4,128,128]{2,1,0:T(8,128)(2,1)S(1)} %copy-done.38), channel_id=1, source_target_pairs={{0,5},{1,4},{2,7},{3,6},{4,1},{5,0},{6,3},{7,2},{8,13},{9,12},{10,... | collective-permute-start | bytes 393224 | tf_op jit(solution)/shard_map/ppermute | solution.py:38
  114.1 9.7 %collective-permute-start.30 = (bf16[4,128,128]{2,1,0:T(8,128)(2,1)S(1)}, bf16[4,128,128]{2,1,0:T(8,128)(2,1)S(1)}, u32[]{:S(2)}, u32[]{:S(2)}) collective-permute-start(bf16[4,128,128]{2,1,0:T(8,128)(2,1)S(1)} %copy-done.37), channel_id=1, source_target_pairs={{0,2},{1,3},{2,4},{3,5},{4,6},{5,7},{6,0},{7,1},{8,10},{9,11},{10,... | collective-permute-start | bytes 393224 | tf_op jit(solution)/shard_map/ppermute | solution.py:38
  115.6 11.0 %collective-permute-start.31 = (bf16[4,128,128]{2,1,0:T(8,128)(2,1)S(1)}, bf16[4,128,128]{2,1,0:T(8,128)(2,1)S(1)}, u32[]{:S(2)}, u32[]{:S(2)}) collective-permute-start(bf16[4,128,128]{2,1,0:T(8,128)(2,1)S(1)} %copy-done.36), channel_id=1, source_target_pairs={{0,3},{1,2},{2,5},{3,4},{4,7},{5,6},{6,1},{7,0},{8,11},{9,10},{10,... | collective-permute-start | bytes 393224 | tf_op jit(solution)/shard_map/ppermute | solution.py:38
  148.8 40.4 %all-to-all-start.1 = ((bf16[16,4,128,128]{3,2,1,0:T(8,128)(2,1)}), bf16[16,4,128,128]{3,2,1,0:T(8,128)(2,1)}, u32[]{:S(2)}, u32[]{:S(2)}) async-start(bf16[16,4,128,128]{3,2,1,0:T(8,128)(2,1)} %bitcast.21), calls=%async_computation.1 | async-start | bytes 4194304 | tf_op jit(solution)/shard_map/all_to_all | solution.py:461
  156.1 5.8 %collective-permute-start.32 = (bf16[4,128,128]{2,1,0:T(8,128)(2,1)S(1)}, bf16[4,128,128]{2,1,0:T(8,128)(2,1)S(1)}, u32[]{:S(2)}, u32[]{:S(2)}) collective-permute-start(bf16[4,128,128]{2,1,0:T(8,128)(2,1)S(1)} %copy-done.49), channel_id=1, source_target_pairs={{0,1},{1,0},{2,3},{3,2},{4,5},{5,4},{6,7},{7,6},{8,9},{9,8},{10,11... | collective-permute-start | bytes 393224 | tf_op jit(solution)/shard_map/ppermute | solution.py:38
  156.2 6.4 %collective-permute-start.33 = (bf16[4,128,128]{2,1,0:T(8,128)(2,1)S(1)}, bf16[4,128,128]{2,1,0:T(8,128)(2,1)S(1)}, u32[]{:S(2)}, u32[]{:S(2)}) collective-permute-start(bf16[4,128,128]{2,1,0:T(8,128)(2,1)S(1)} %copy-done.48), channel_id=1, source_target_pairs={{0,6},{1,7},{2,0},{3,1},{4,2},{5,3},{6,4},{7,5},{8,14},{9,15},{10,... | collective-permute-start | bytes 393224 | tf_op jit(solution)/shard_map/ppermute | solution.py:38
  156.8 7.5 %collective-permute-start.34 = (bf16[4,128,128]{2,1,0:T(8,128)(2,1)S(1)}, bf16[4,128,128]{2,1,0:T(8,128)(2,1)S(1)}, u32[]{:S(2)}, u32[]{:S(2)}) collective-permute-start(bf16[4,128,128]{2,1,0:T(8,128)(2,1)S(1)} %copy-done.47), channel_id=1, source_target_pairs={{0,7},{1,6},{2,1},{3,0},{4,3},{5,2},{6,5},{7,4},{8,15},{9,14},{10,... | collective-permute-start | bytes 393224 | tf_op jit(solution)/shard_map/ppermute | solution.py:38
  158.8 7.9 %collective-permute-start.35 = (bf16[4,128,128]{2,1,0:T(8,128)(2,1)S(1)}, bf16[4,128,128]{2,1,0:T(8,128)(2,1)S(1)}, u32[]{:S(2)}, u32[]{:S(2)}) collective-permute-start(bf16[4,128,128]{2,1,0:T(8,128)(2,1)S(1)} %copy-done.45), channel_id=1, source_target_pairs={{0,4},{1,5},{2,6},{3,7},{4,0},{5,1},{6,2},{7,3},{8,12},{9,13},{10,... | collective-permute-start | bytes 393224 | tf_op jit(solution)/shard_map/ppermute | solution.py:38
  160.2 8.2 %collective-permute-start.36 = (bf16[4,128,128]{2,1,0:T(8,128)(2,1)S(1)}, bf16[4,128,128]{2,1,0:T(8,128)(2,1)S(1)}, u32[]{:S(2)}, u32[]{:S(2)}) collective-permute-start(bf16[4,128,128]{2,1,0:T(8,128)(2,1)S(1)} %copy-done.44), channel_id=1, source_target_pairs={{0,5},{1,4},{2,7},{3,6},{4,1},{5,0},{6,3},{7,2},{8,13},{9,12},{10,... | collective-permute-start | bytes 393224 | tf_op jit(solution)/shard_map/ppermute | solution.py:38
  162.0 9.7 %collective-permute-start.37 = (bf16[4,128,128]{2,1,0:T(8,128)(2,1)S(1)}, bf16[4,128,128]{2,1,0:T(8,128)(2,1)S(1)}, u32[]{:S(2)}, u32[]{:S(2)}) collective-permute-start(bf16[4,128,128]{2,1,0:T(8,128)(2,1)S(1)} %copy-done.43), channel_id=1, source_target_pairs={{0,2},{1,3},{2,4},{3,5},{4,6},{5,7},{6,0},{7,1},{8,10},{9,11},{10,... | collective-permute-start | bytes 393224 | tf_op jit(solution)/shard_map/ppermute | solution.py:38
  162.7 11.7 %collective-permute-start.38 = (bf16[4,128,128]{2,1,0:T(8,128)(2,1)S(1)}, bf16[4,128,128]{2,1,0:T(8,128)(2,1)S(1)}, u32[]{:S(2)}, u32[]{:S(2)}) collective-permute-start(bf16[4,128,128]{2,1,0:T(8,128)(2,1)S(1)} %copy-done.41), channel_id=1, source_target_pairs={{0,3},{1,2},{2,5},{3,4},{4,7},{5,6},{6,1},{7,0},{8,11},{9,10},{10,... | collective-permute-start | bytes 393224 | tf_op jit(solution)/shard_map/ppermute | solution.py:38
  (43 other events, 437.1 us)
where the time goes:
time: 224 us; the launch traced here: 223 us
  waiting for transfers between devices  72.8 us (32%)
  Pallas kernels  58.6 us (26%)
  starting transfers between devices  57.5 us (26%)
  blocking collectives  19.7 us (9%)
  local copies, waits for them, and re-layouts  8.74 us (4%)
  other arithmetic  4.4 us (2%)
    ppermute x21, waiting for transfers between devices, shifted(): return lax.ppermute(value, axis, [(i, (i + step) % 4) for i in range(4)])  46.5 us
    ppermute x21, starting transfers between devices, shifted(): return lax.ppermute(value, axis, [(i, (i + step) % 4) for i in range(4)])  31.5 us
    ppermute x14, waiting for transfers between devices, to_peer(): return lax.ppermute(value, JA, moves)  23.1 us
    pallas_call x2, Pallas kernels, steps(): pl.pallas_call(second_kind_kernel, out_shape=block, in_specs=[SMEM] * 3 +...  21.6 us
    all_to_all x1, blocking collectives, steps(): got = lax.all_to_all(split, ALL, split_axis=0, concat_axis=0, tiled=True)  19.7 us
    ppermute x14, starting transfers between devices, to_peer(): return lax.ppermute(value, JA, moves)  12.8 us
    all_to_all x2, starting transfers between devices, steps(): lax.all_to_all(send_i.reshape(16, 4, pno, pno), IA, split_axis=0, concat_...  12.6 us
    pallas_call x1, Pallas kernels, steps(): pl.pallas_call(functools.partial(last_kernel, factor), out_shape=[block,...  12.1 us
  transfers between devices with their start and end apart: 41, of which 22 were waited for; matrix products, arithmetic and copies ran while one was open for 2% of the time, Pallas kernels for 12%

commit v1 on v0

--- a/solution.py
+++ b/solution.py
@@ -162,9 +162,10 @@
             ref[r] = sent[asked_j[peer, r]]
 
 
-def exchange_kernel(where, second, dom, asked_j, coef_t, projected, scale, *refs):
+def exchange_kernel(where, second, dom, asked_j, coef_far, projected_far, scale_far, *refs):
     pieces, (exch, asked, send_i), send_j = refs[:16], refs[16:19], refs[19:27]
-    rows, sems, tiles, tile_sem, sent, asked_i, asked_sem = refs[27:]
+    rows, sems, tiles, tile_sem, sent, asked_i, asked_sem = refs[27:34]
+    coef_t, projected, scale, load_sem = refs[34:]
     y, x = where[0], where[1]
     units = (2 * BLK + 16, 2 * BLK)
 
@@ -193,6 +194,8 @@
         )
         copies[-1].start()
     lax.fori_loop(0, exch.shape[0], start, 0)
+    arrays = [(coef_far, coef_t), (projected_far, projected), (scale_far, scale)]
+    loads = Loads([], arrays, load_sem)
     for copy in copies:
         copy.wait()
 
@@ -212,7 +215,7 @@
             exch[p] = value
             sent[p] = (value * scale[p]).astype(BF16)
 
-    in_groups(exch.shape[0], one)
+    loads.each_group(one)
     to_scalars.wait()
     pack(sent, where, asked_i, asked_j, send_i, send_j)
 
@@ -309,10 +312,10 @@
     loads.each_group(step)
 
 
-def first_kind(loaded, link, couple):
+def first_kind(loaded, link, couple, extra=()):
     margin_far, table_far, base_far, scale_far, margin, table, base, scale, sem = loaded
     arrays = [(margin_far, margin), (base_far, base), (scale_far, scale)]
-    loads = Loads([(table_far, table)], arrays, sem)
+    loads = Loads([(table_far, table)], arrays + list(extra), sem)
 
     def values(group):
         totals = couplings(group, margin, table, lambda p, n: link[p, n], couple)
@@ -333,9 +336,10 @@
     pack(sent, where, asked_i, asked_j, send_i, send_j)
 
 
-def last_kernel(factor, link, couple, dom, coef, *refs):
+def last_kernel(factor, link, couple, dom, coef_far, *refs):
     far, (amp, dens, acc) = refs[:4], refs[4:7]
-    loads, values = first_kind(far + refs[7:], link, couple)
+    coef = refs[12]
+    loads, values = first_kind(far + refs[7:12], link, couple, [(coef_far, coef)])
     acc[...] = jnp.zeros_like(acc)
 
     def step(group):
@@ -431,7 +435,7 @@
     exch, asked_i, *sends = pl.pallas_call(
         exchange_kernel,
         out_shape=[block, jax.ShapeDtypeStruct((16, BLK), jnp.int32)] + send_types,
-        in_specs=[SMEM] * 4 + [WHOLE] * 3 + [FAR] * 16,
+        in_specs=[SMEM] * 4 + [FAR] * 19,
         out_specs=[WHOLE] * 11,
         scratch_shapes=fetched
         + [
@@ -440,6 +444,10 @@
             pltpu.VMEM((pairs, pno, pno), BF16),
             pltpu.SMEM((16, BLK), jnp.int32),
             pltpu.SemaphoreType.DMA,
+            pltpu.VMEM((pairs, pno, domain), BF16),
+            pltpu.VMEM((pairs, pno, aux), BF16),
+            pltpu.VMEM((pairs, pno, pno), F32),
+            pltpu.SemaphoreType.DMA((3 * GROUPS,)),
         ],
         compiler_params=params(),
         cost_estimate=cost(pairs * pno * domain * aux * 3, 10 << 20),
@@ -454,7 +462,7 @@
         pltpu.VMEM((64, pno, pno), BF16),
         values,
         values,
-        pltpu.SemaphoreType.DMA((1 + 3 * GROUPS,)),
+        pltpu.SemaphoreType.DMA((1 + 4 * GROUPS,)),
     ]
     for iteration in range(ITERS):
         send_i, send_j = sends[0], sends[1:]
@@ -497,9 +505,11 @@
             amplitudes, partial_sum = pl.pallas_call(
                 functools.partial(last_kernel, factor),
                 out_shape=[block, jax.ShapeDtypeStruct((pao, pao), BF16)],
-                in_specs=[SMEM] * 3 + [WHOLE] + [FAR] * 4,
+                in_specs=[SMEM] * 3 + [FAR] * 5,
                 out_specs=[WHOLE] * 2,
-                scratch_shapes=[pltpu.VMEM((4, 4, BLK, BLK), F32)] + first_scratch,
+                scratch_shapes=[pltpu.VMEM((4, 4, BLK, BLK), F32)]
+                + first_scratch
+                + [pltpu.VMEM((pairs, domain, pno), BF16)],
                 compiler_params=params(),
                 cost_estimate=cost(work, 16 << 20),
                 name="couple_last",

time: 224 us -> 224 us (level)
  no operation moved by 1% of the time
where the time goes in v1:
time: 224 us; the launch traced here: 223 us
  waiting for transfers between devices  72.8 us (32%)
  Pallas kernels  58.8 us (26%)
  starting transfers between devices  57.5 us (26%)
  blocking collectives  19.7 us (9%)
  local copies, waits for them, and re-layouts  8.74 us (4%)
  other arithmetic  4.4 us (2%)
    ppermute x21, waiting for transfers between devices, shifted(): return lax.ppermute(value, axis, [(i, (i + step) % 4) for i in range(4)])  46.5 us
    ppermute x21, starting transfers between devices, shifted(): return lax.ppermute(value, axis, [(i, (i + step) % 4) for i in range(4)])  31.5 us
    ppermute x14, waiting for transfers between devices, to_peer(): return lax.ppermute(value, JA, moves)  23.1 us
    pallas_call x2, Pallas kernels, steps(): pl.pallas_call(second_kind_kernel, out_shape=block, in_specs=[SMEM] * 3 +...  21.6 us
    all_to_all x1, blocking collectives, steps(): got = lax.all_to_all(split, ALL, split_axis=0, concat_axis=0, tiled=True)  19.7 us
    ppermute x14, starting transfers between devices, to_peer(): return lax.ppermute(value, JA, moves)  12.8 us
    all_to_all x2, starting transfers between devices, steps(): lax.all_to_all(send_i.reshape(16, 4, pno, pno), IA, split_axis=0, concat_...  12.6 us
    pallas_call x1, Pallas kernels, steps(): pl.pallas_call(functools.partial(last_kernel, factor), out_shape=[block,...  12 us
  transfers between devices with their start and end apart: 41, of which 22 were waited for; matrix products, arithmetic and copies ran while one was open for 2% of the time, Pallas kernels for 12%

profile of v1, /device:TPU:0, one launch (start us, length us, event | category | flops | bytes accessed | tf_op | source)
XLA Modules:
  0.0 223.2 jit_solution(10792330227807682519)
XLA Ops:
  0.6 1.1 slice_bitcast_fusion
  3.3 2.9 %collective-permute-start.8 = (bf16[272,512]{1,0:T(8,128)(2,1)}, bf16[272,512]{1,0:T(8,128)(2,1)}, u32[]{:S(2)}, u32[]{:S(2)}) collective-permute-start(bf16[272,512]{1,0:T(8,128)(2,1)} %pad_maximum_fusion.2), channel_id=1, source_target_pairs={{0,24},{8,0},{16,8},{24,16},{1,25},{9,1},{17,9},{25,17},{2,26},{10... | collective-permute-start | bytes 835592 | tf_op jit(solution)/shard_map/ppermute | solution.py:31
  7.0 3.0 %collective-permute-start.17 = (bf16[256,512]{1,0:T(8,128)(2,1)S(1)}, bf16[256,512]{1,0:T(8,128)(2,1)S(1)}, u32[]{:S(2)}, u32[]{:S(2)}) collective-permute-start(bf16[256,512]{1,0:T(8,128)(2,1)S(1)} %get-tuple-element.50), channel_id=1, source_target_pairs={{0,96},{32,0},{64,32},{96,64},{1,97},{33,1},{65,33},{97,65},{2,98}... | collective-permute-start | bytes 786440 | tf_op jit(solution)/shard_map/ppermute | solution.py:31
  11.7 8.9 %collective-permute-done.17 = bf16[256,512]{1,0:T(8,128)(2,1)S(1)} collective-permute-done((bf16[256,512]{1,0:T(8,128)(2,1)S(1)}, bf16[256,512]{1,0:T(8,128)(2,1)S(1)}, u32[]{:S(2)}, u32[]{:S(2)}) %collective-permute-start.17) | collective-permute-done | bytes 262176 | tf_op jit(solution)/shard_map/ppermute | solution.py:31
  20.6 1.9 collective-permute-start
  22.5 2.2 collective-permute-start.1
  24.7 3.5 %collective-permute-start.2 = (bf16[528,512]{1,0:T(8,128)(2,1)S(1)}, bf16[528,512]{1,0:T(8,128)(2,1)S(1)}, u32[]{:S(2)}, u32[]{:S(2)}) collective-permute-start(bf16[528,512]{1,0:T(8,128)(2,1)S(1)} %fusion.1.refs_0_), channel_id=1, source_target_pairs={{0,4},{2,6},{4,0},{6,2},{1,5},{3,7},{5,1},{7,3},{8,12},{10,14},{12... | collective-permute-start | bytes 1622024 | tf_op jit(solution)/shard_map/ppermute | solution.py:31
  29.3 1.3 constant_dynamic-update-slice_fusion.1
  30.6 8.2 %collective-permute-done.7 = bf16[272,512]{1,0:T(8,128)(2,1)S(1)} collective-permute-done((bf16[272,512]{1,0:T(8,128)(2,1)}, bf16[272,512]{1,0:T(8,128)(2,1)S(1)}, u32[]{:S(2)}, u32[]{:S(2)}) %collective-permute-start.7) | collective-permute-done | bytes 278560 | tf_op jit(solution)/shard_map/ppermute | solution.py:31
  39.1 1.7 collective-permute-start.19
  40.9 3.4 %collective-permute-done.1.refs_2_ = bf16[528,512]{1,0:T(8,128)(2,1)S(1)} collective-permute-done((bf16[528,512]{1,0:T(8,128)(2,1)S(1)}, bf16[528,512]{1,0:T(8,128)(2,1)S(1)}, u32[]{:S(2)}, u32[]{:S(2)}) %collective-permute-start.1) | collective-permute-done | bytes 540704 | tf_op jit(solution)/shard_map/ppermute | solution.py:31
  44.2 4.3 %collective-permute-start.13 = (bf16[544,512]{1,0:T(8,128)(2,1)S(1)}, bf16[544,512]{1,0:T(8,128)(2,1)}, u32[]{:S(2)}, u32[]{:S(2)}) collective-permute-start(bf16[544,512]{1,0:T(8,128)(2,1)S(1)} %constant_dynamic-update-slice_fusion.refs_1_), channel_id=1, source_target_pairs={{0,96},{32,0},{64,32},{96,64},{1,97},{33,1},{65,33},{97,65},{2,98}... | collective-permute-start | bytes 1671176 | tf_op jit(solution)/shard_map/ppermute | solution.py:31
  50.2 2.4 %collective-permute-start.21 = (bf16[512,512]{1,0:T(8,128)(2,1)S(1)}, bf16[512,512]{1,0:T(8,128)(2,1)S(1)}, u32[]{:S(2)}, u32[]{:S(2)}) collective-permute-start(bf16[512,512]{1,0:T(8,128)(2,1)S(1)} %pad_maximum_fusion.1.refs_8_), channel_id=1, source_target_pairs={{0,24},{8,0},{16,8},{24,16},{1,25},{9,1},{17,9},{25,17},{2,26},{10... | collective-permute-start | bytes 1572872 | tf_op jit(solution)/shard_map/ppermute | solution.py:31
  52.7 1.0 collective-permute-done.22.refs_13_
  53.7 1.6 collective-permute-done.19.refs_10_
  55.3 9.8 %collective-permute-done.20.refs_11_ = bf16[512,512]{1,0:T(8,128)(2,1)S(1)} collective-permute-done((bf16[512,512]{1,0:T(8,128)(2,1)S(1)}, bf16[512,512]{1,0:T(8,128)(2,1)S(1)}, u32[]{:S(2)}, u32[]{:S(2)}) %collective-permute-start.20) | collective-permute-done | bytes 524320 | tf_op jit(solution)/shard_map/ppermute | solution.py:31
  65.7 4.7 %collective-permute-done.11.refs_3_ = bf16[544,512]{1,0:T(8,128)(2,1)S(1)} collective-permute-done((bf16[544,512]{1,0:T(8,128)(2,1)S(1)}, bf16[544,512]{1,0:T(8,128)(2,1)S(1)}, u32[]{:S(2)}, u32[]{:S(2)}) %collective-permute-start.11) | collective-permute-done | bytes 557088 | tf_op jit(solution)/shard_map/ppermute | solution.py:31
  71.2 7.7 %collective-permute-done.10.refs_2_ = bf16[544,512]{1,0:T(8,128)(2,1)} collective-permute-done((bf16[544,512]{1,0:T(8,128)(2,1)S(1)}, bf16[544,512]{1,0:T(8,128)(2,1)}, u32[]{:S(2)}, u32[]{:S(2)}) %collective-permute-start.10) | collective-permute-done | bytes 557088 | tf_op jit(solution)/shard_map/ppermute | solution.py:31
  79.0 1.2 collective-permute-start.15
  81.1 2.2 collective-permute-start.24
  84.8 1.3 copy.17
  86.7 1.4 add_divide_fusion.scale_far.refs_3_
  88.1 5.7 %project_first.1 = (bf16[16,128,512]{2,1,0:T(8,128)(2,1)}, s32[8,128]{1,0:T(8,128)}) custom-call(s32[4]{0:T(128)} %pad_add_fusion.where, s32[16]{0:T(128)} %first.1, s32[16,2]{1,0:T(8,128)} %copy.22.dom, bf16[16,128,256]{2,1,0:T(8,128)(2,1)} %bitcast.18, bf16[528,512]{1,0:T(8,128)(2,1)} %copy-done.2, bf16[528,512]{1,0:T(8,128)(2,1)} %copy-done.9, ...), custom_call_target="tpu_custom_call" | custom-call | flops 536870912 | bytes 6291456 | tf_op jit(solution)/shard_map/project_first/pallas_call | solution.py:420
  93.9 1.2 collective-permute-done.23.refs_14_
  95.0 8.6 %exchange.1 = (f32[16,128,128]{2,1,0:T(8,128)}, s32[16,128]{1,0:T(8,128)}, bf16[64,128,128]{2,1,0:T(8,128)(2,1)}, bf16[4,128,128]{2,1,0:T(8,128)(2,1)}, bf16[4,1...) custom-call(s32[4]{0:T(128)} %pad_add_fusion.where, ...), custom_call_target="tpu_custom_call" | custom-call | flops 805306368 | bytes 10485760 | tf_op jit(solution)/shard_map/exchange/pallas_call | solution.py:435
  103.7 5.2 %all-to-all-start = ((bf16[16,4,128,128]{3,2,1,0:T(8,128)(2,1)}), bf16[16,4,128,128]{3,2,1,0:T(8,128)(2,1)}, u32[]{:S(2)}, u32[]{:S(2)}) async-start(bf16[16,4,128,128]{3,2,1,0:T(8,128)(2,1)} %bitcast.20), calls=%async_computation | async-start | bytes 4194304 | tf_op jit(solution)/shard_map/all_to_all | solution.py:469
  110.9 2.1 collective-permute-start.28
  113.0 1.3 collective-permute-start.29
  117.1 1.7 collective-permute-done.28.refs_4_
  118.8 2.0 collective-permute-done.29.refs_5_
  120.8 3.2 %collective-permute-done.30.refs_6_ = bf16[4,128,128]{2,1,0:T(8,128)(2,1)S(1)} collective-permute-done((bf16[4,128,128]{2,1,0:T(8,128)(2,1)S(1)}, bf16[4,128,128]{2,1,0:T(8,128)(2,1)S(1)}, u32[]{:S(2)}, u32[]{:S(2)}) %collective-permute-start.30) | collective-permute-done | bytes 131104 | tf_op jit(solution)/shard_map/ppermute | solution.py:38
  124.0 2.7 %collective-permute-done.31.refs_7_ = bf16[4,128,128]{2,1,0:T(8,128)(2,1)S(1)} collective-permute-done((bf16[4,128,128]{2,1,0:T(8,128)(2,1)S(1)}, bf16[4,128,128]{2,1,0:T(8,128)(2,1)S(1)}, u32[]{:S(2)}, u32[]{:S(2)}) %collective-permute-start.31) | collective-permute-done | bytes 131104 | tf_op jit(solution)/shard_map/ppermute | solution.py:38
  127.3 10.7 %couple_second.2.refs_2_ = f32[16,128,128]{2,1,0:T(8,128)} custom-call(s32[4]{0:T(128)} %pad_add_fusion.where, s32[16,16]{1,0:T(8,128)} %link.6, f32[16,16]{1,0:T(8,128)} %couple.6, bf16[16,16,128,128]{3,2,1,0:T(8,128)(2,1)} %margin_far.3, f32[16,128,128]{2,1,0:T(8,128)} %get-tuple-element.30.exch_far, bf16[4,128,128]{2,1,0:T(8,128)(2,1)} %get-tuple-element.31.refs_0_, ...), custom_call_target="tpu_custom_call" | custom-call | flops 2147483648 | bytes 12582912 | tf_op jit(solution)/shard_map/couple_second/pallas_call | solution.py:476
  138.1 10.8 %couple_first.1 = (bf16[64,128,128]{2,1,0:T(8,128)(2,1)}, bf16[4,128,128]{2,1,0:T(8,128)(2,1)}, bf16[4,128,128]{2,1,0:T(8,128)(2,1)}, bf16[4,128,128]{2,1,0:T(8,...) custom-call(s32[4]{0:T(128)} %pad_add_fusion.where, ...), custom_call_target="tpu_custom_call" | custom-call | flops 2147483648 | bytes 14680064 | tf_op jit(solution)/shard_map/couple_first/pallas_call | solution.py:493
  149.0 7.4 %all-to-all-start.1 = ((bf16[16,4,128,128]{3,2,1,0:T(8,128)(2,1)}), bf16[16,4,128,128]{3,2,1,0:T(8,128)(2,1)}, u32[]{:S(2)}, u32[]{:S(2)}) async-start(bf16[16,4,128,128]{3,2,1,0:T(8,128)(2,1)} %bitcast.21), calls=%async_computation.1 | async-start | bytes 4194304 | tf_op jit(solution)/shard_map/all_to_all | solution.py:469
  157.1 1.9 collective-permute-start.34
  159.0 1.4 collective-permute-start.35
  160.4 1.8 collective-permute-start.36
  163.4 1.2 collective-permute-done.34.refs_3_
  164.6 2.3 %collective-permute-done.35.refs_4_ = bf16[4,128,128]{2,1,0:T(8,128)(2,1)S(1)} collective-permute-done((bf16[4,128,128]{2,1,0:T(8,128)(2,1)S(1)}, bf16[4,128,128]{2,1,0:T(8,128)(2,1)S(1)}, u32[]{:S(2)}, u32[]{:S(2)}) %collective-permute-start.35) | collective-permute-done | bytes 131104 | tf_op jit(solution)/shard_map/ppermute | solution.py:38
  166.9 1.7 collective-permute-done.36.refs_5_
  168.5 3.4 %collective-permute-done.37.refs_6_ = bf16[4,128,128]{2,1,0:T(8,128)(2,1)S(1)} collective-permute-done((bf16[4,128,128]{2,1,0:T(8,128)(2,1)S(1)}, bf16[4,128,128]{2,1,0:T(8,128)(2,1)S(1)}, u32[]{:S(2)}, u32[]{:S(2)}) %collective-permute-start.37) | collective-permute-done | bytes 131104 | tf_op jit(solution)/shard_map/ppermute | solution.py:38
  171.9 2.7 %collective-permute-done.38.refs_7_ = bf16[4,128,128]{2,1,0:T(8,128)(2,1)S(1)} collective-permute-done((bf16[4,128,128]{2,1,0:T(8,128)(2,1)S(1)}, bf16[4,128,128]{2,1,0:T(8,128)(2,1)S(1)}, u32[]{:S(2)}, u32[]{:S(2)}) %collective-permute-start.38) | collective-permute-done | bytes 131104 | tf_op jit(solution)/shard_map/ppermute | solution.py:38
  175.3 10.8 %couple_second.3.refs_2_ = f32[16,128,128]{2,1,0:T(8,128)} custom-call(s32[4]{0:T(128)} %pad_add_fusion.where, s32[16,16]{1,0:T(8,128)} %link.6, f32[16,16]{1,0:T(8,128)} %couple.6, bf16[16,16,128,128]{3,2,1,0:T(8,128)(2,1)} %margin_far.3, f32[16,128,128]{2,1,0:T(8,128)} %get-tuple-element.30.exch_far, bf16[4,128,128]{2,1,0:T(8,128)(2,1)} %get-tuple-element.40.refs_0_, ...), custom_call_target="tpu_custom_call" | custom-call | flops 2147483648 | bytes 12582912 | tf_op jit(solution)/shard_map/couple_second/pallas_call | solution.py:476
  186.1 3.3 %all-to-all-done.1 = bf16[16,4,128,128]{3,2,1,0:T(8,128)(2,1)} async-done(((bf16[16,4,128,128]{3,2,1,0:T(8,128)(2,1)}), bf16[16,4,128,128]{3,2,1,0:T(8,128)(2,1)}, u32[]{:S(2)}, u32[]{:S(2)}) %all-to-all-start.1) | async-done | bytes 2097184 | tf_op jit(solution)/shard_map/all_to_all | solution.py:469
  189.4 12.0 %couple_last.1 = (f32[16,128,128]{2,1,0:T(8,128)}, bf16[512,512]{1,0:T(8,128)(2,1)}) custom-call(s32[16,16]{1,0:T(8,128)} %link.7, f32[16,16]{1,0:T(8,128)} %couple.7, s32[16,2]{1,0:T(8,128)} %copy.22.dom, bf16[16,256,128]{2,1,0:T(8,128)(2,1)} %coef_far.1, bf16[16,16,128,128]{3,2,1,0:T(8,128)(2,1)} %refs_0_.3, bf16[64,128,128]{2,1,0:T(8,128)(2,1)} %bitcast.13.refs_1_, ...), custom_call_target="tpu_custom_call" | custom-call | flops 2147483648 | bytes 16777216 | tf_op jit(solution)/shard_map/couple_last/pallas_call | solution.py:505
  201.4 1.2 reshape.36
  202.6 19.7 %all_to_all.15 = bf16[128,4,512]{2,1,0:T(4,128)(2,1)S(1)} all-to-all(bf16[128,4,512]{2,1,0:T(4,128)(2,1)S(1)} %reshape.36), channel_id=1, replica_groups=mesh['y'=4,'x'=4,'z'=4,'c'=2] {'y','x','z','c'}, dimensions={0} | all-to-all | bytes 1048576 | tf_op jit(solution)/shard_map/all_to_all | solution.py:518
  (161 shorter events, 20.5 us)
Async XLA Ops:
  3.3 24.9 %collective-permute-start.8 = (bf16[272,512]{1,0:T(8,128)(2,1)}, bf16[272,512]{1,0:T(8,128)(2,1)}, u32[]{:S(2)}, u32[]{:S(2)}) collective-permute-start(bf16[272,512]{1,0:T(8,128)(2,1)} %pad_maximum_fusion.2), channel_id=1, source_target_pairs={{0,24},{8,0},{16,8},{24,16},{1,25},{9,1},{17,9},{25,17},{2,26},{10... | collective-permute-start | bytes 835592 | tf_op jit(solution)/shard_map/ppermute | solution.py:31
  6.2 22.1 %collective-permute-start.9 = (bf16[272,512]{1,0:T(8,128)(2,1)}, bf16[272,512]{1,0:T(8,128)(2,1)S(1)}, u32[]{:S(2)}, u32[]{:S(2)}) collective-permute-start(bf16[272,512]{1,0:T(8,128)(2,1)} %pad_maximum_fusion.2), channel_id=1, source_target_pairs={{0,16},{8,24},{16,0},{24,8},{1,17},{9,25},{17,1},{25,9},{2,18},{10... | collective-permute-start | bytes 835592 | tf_op jit(solution)/shard_map/ppermute | solution.py:31
  7.0 13.6 %collective-permute-start.17 = (bf16[256,512]{1,0:T(8,128)(2,1)S(1)}, bf16[256,512]{1,0:T(8,128)(2,1)S(1)}, u32[]{:S(2)}, u32[]{:S(2)}) collective-permute-start(bf16[256,512]{1,0:T(8,128)(2,1)S(1)} %get-tuple-element.50), channel_id=1, source_target_pairs={{0,96},{32,0},{64,32},{96,64},{1,97},{33,1},{65,33},{97,65},{2,98}... | collective-permute-start | bytes 786440 | tf_op jit(solution)/shard_map/ppermute | solution.py:31
  10.0 12.5 %collective-permute-start.18 = (bf16[256,512]{1,0:T(8,128)(2,1)S(1)}, bf16[256,512]{1,0:T(8,128)(2,1)S(1)}, u32[]{:S(2)}, u32[]{:S(2)}) collective-permute-start(bf16[256,512]{1,0:T(8,128)(2,1)S(1)} %get-tuple-element.50), channel_id=1, source_target_pairs={{0,64},{32,96},{64,0},{96,32},{1,65},{33,97},{65,1},{97,33},{2,66}... | collective-permute-start | bytes 786440 | tf_op jit(solution)/shard_map/ppermute | solution.py:31
  10.6 14.1 %collective-permute-start.16 = (bf16[256,512]{1,0:T(8,128)(2,1)S(1)}, bf16[256,512]{1,0:T(8,128)(2,1)S(1)}, u32[]{:S(2)}, u32[]{:S(2)}) collective-permute-start(bf16[256,512]{1,0:T(8,128)(2,1)S(1)} %get-tuple-element.50), channel_id=1, source_target_pairs={{0,32},{32,64},{64,96},{96,0},{1,33},{33,65},{65,97},{97,1},{2,34}... | collective-permute-start | bytes 786440 | tf_op jit(solution)/shard_map/ppermute | solution.py:31
  20.6 18.5 %collective-permute-start = (bf16[528,512]{1,0:T(8,128)(2,1)S(1)}, bf16[528,512]{1,0:T(8,128)(2,1)S(1)}, u32[]{:S(2)}, u32[]{:S(2)}) collective-permute-start(bf16[528,512]{1,0:T(8,128)(2,1)S(1)} %fusion.1.refs_0_), channel_id=1, source_target_pairs={{0,2},{2,4},{4,6},{6,0},{1,3},{3,5},{5,7},{7,1},{8,10},{10,12},{12... | collective-permute-start | bytes 1622024 | tf_op jit(solution)/shard_map/ppermute | solution.py:31
  22.5 21.7 %collective-permute-start.1 = (bf16[528,512]{1,0:T(8,128)(2,1)S(1)}, bf16[528,512]{1,0:T(8,128)(2,1)S(1)}, u32[]{:S(2)}, u32[]{:S(2)}) collective-permute-start(bf16[528,512]{1,0:T(8,128)(2,1)S(1)} %fusion.1.refs_0_), channel_id=1, source_target_pairs={{0,6},{2,0},{4,2},{6,4},{1,7},{3,1},{5,3},{7,5},{8,14},{10,8},{12,... | collective-permute-start | bytes 1622024 | tf_op jit(solution)/shard_map/ppermute | solution.py:31
  24.7 23.8 %collective-permute-start.2 = (bf16[528,512]{1,0:T(8,128)(2,1)S(1)}, bf16[528,512]{1,0:T(8,128)(2,1)S(1)}, u32[]{:S(2)}, u32[]{:S(2)}) collective-permute-start(bf16[528,512]{1,0:T(8,128)(2,1)S(1)} %fusion.1.refs_0_), channel_id=1, source_target_pairs={{0,4},{2,6},{4,0},{6,2},{1,5},{3,7},{5,1},{7,3},{8,12},{10,14},{12... | collective-permute-start | bytes 1622024 | tf_op jit(solution)/shard_map/ppermute | solution.py:31
  28.2 21.2 %collective-permute-start.3 = (bf16[528,512]{1,0:T(8,128)(2,1)S(1)}, bf16[528,512]{1,0:T(8,128)(2,1)S(1)}, u32[]{:S(2)}, u32[]{:S(2)}) collective-permute-start(bf16[528,512]{1,0:T(8,128)(2,1)S(1)} %fusion.1.refs_0_), channel_id=1, source_target_pairs={{0,1},{1,0},{2,3},{3,2},{4,5},{5,4},{6,7},{7,6},{8,9},{9,8},{10,11... | collective-permute-start | bytes 1622024 | tf_op jit(solution)/shard_map/ppermute | solution.py:67
  28.2 10.6 %collective-permute-start.7 = (bf16[272,512]{1,0:T(8,128)(2,1)}, bf16[272,512]{1,0:T(8,128)(2,1)S(1)}, u32[]{:S(2)}, u32[]{:S(2)}) collective-permute-start(bf16[272,512]{1,0:T(8,128)(2,1)} %pad_maximum_fusion.2), channel_id=1, source_target_pairs={{0,8},{8,16},{16,24},{24,0},{1,9},{9,17},{17,25},{25,1},{2,10},{10... | collective-permute-start | bytes 835592 | tf_op jit(solution)/shard_map/ppermute | solution.py:31
  29.3 54.8 %copy-start.34 = (s32[16,2]{0,1:T(2,128)S(1)}, s32[16,2]{0,1:T(2,128)}, u32[]{:S(2)}) copy-start(s32[16,2]{0,1:T(2,128)} %param.17) | copy-start | bytes 388
  29.3 55.5 %copy-start = (bf16[16,256,128]{2,1,0:T(8,128)(2,1)S(1)}, bf16[16,256,128]{2,1,0:T(8,128)(2,1)}, u32[]{:S(2)}) copy-start(bf16[16,256,128]{2,1,0:T(8,128)(2,1)} %coef_far.1) | copy-start | bytes 3145732
  38.8 14.9 %collective-permute-start.22 = (bf16[512,512]{1,0:T(8,128)(2,1)S(1)}, bf16[512,512]{1,0:T(8,128)(2,1)}, u32[]{:S(2)}, u32[]{:S(2)}) collective-permute-start(bf16[512,512]{1,0:T(8,128)(2,1)S(1)} %constant_dynamic-update-slice_fusion.2.refs_9_), channel_id=1, source_target_pairs={{0,24},{8,0},{16,8},{24,16},{1,25},{9,1},{17,9},{25,17},{2,26},{10... | collective-permute-start | bytes 1572872 | tf_op jit(solution)/shard_map/ppermute | solution.py:31
  39.1 41.0 %copy-start.9 = (bf16[528,512]{1,0:T(8,128)(2,1)}, bf16[528,512]{1,0:T(8,128)(2,1)S(1)}, u32[]{:S(2)}) copy-start(bf16[528,512]{1,0:T(8,128)(2,1)S(1)} %collective-permute-done.refs_1_) | copy-start | bytes 1622020
  39.1 16.1 %collective-permute-start.19 = (bf16[512,512]{1,0:T(8,128)(2,1)S(1)}, bf16[512,512]{1,0:T(8,128)(2,1)}, u32[]{:S(2)}, u32[]{:S(2)}) collective-permute-start(bf16[512,512]{1,0:T(8,128)(2,1)S(1)} %pad_maximum_fusion.1.refs_8_), channel_id=1, source_target_pairs={{0,8},{8,16},{16,24},{24,0},{1,9},{9,17},{17,25},{25,1},{2,10},{10... | collective-permute-start | bytes 1572872 | tf_op jit(solution)/shard_map/ppermute | solution.py:31
  40.8 45.2 %copy-start.5 = (bf16[544,512]{1,0:T(8,128)(2,1)}, bf16[544,512]{1,0:T(8,128)(2,1)S(1)}, u32[]{:S(2)}) copy-start(bf16[544,512]{1,0:T(8,128)(2,1)S(1)} %constant_dynamic-update-slice_fusion.refs_1_) | copy-start | bytes 1671172
  44.2 35.9 %copy-start.10 = (bf16[528,512]{1,0:T(8,128)(2,1)}, bf16[528,512]{1,0:T(8,128)(2,1)S(1)}, u32[]{:S(2)}) copy-start(bf16[528,512]{1,0:T(8,128)(2,1)S(1)} %collective-permute-done.1.refs_2_) | copy-start | bytes 1622020
  44.2 21.3 %collective-permute-start.13 = (bf16[544,512]{1,0:T(8,128)(2,1)S(1)}, bf16[544,512]{1,0:T(8,128)(2,1)}, u32[]{:S(2)}, u32[]{:S(2)}) collective-permute-start(bf16[544,512]{1,0:T(8,128)(2,1)S(1)} %constant_dynamic-update-slice_fusion.refs_1_), channel_id=1, source_target_pairs={{0,96},{32,0},{64,32},{96,64},{1,97},{33,1},{65,33},{97,65},{2,98}... | collective-permute-start | bytes 1671176 | tf_op jit(solution)/shard_map/ppermute | solution.py:31
  48.5 16.5 %collective-permute-start.20 = (bf16[512,512]{1,0:T(8,128)(2,1)S(1)}, bf16[512,512]{1,0:T(8,128)(2,1)S(1)}, u32[]{:S(2)}, u32[]{:S(2)}) collective-permute-start(bf16[512,512]{1,0:T(8,128)(2,1)S(1)} %constant_dynamic-update-slice_fusion.2.refs_9_), channel_id=1, source_target_pairs={{0,8},{8,16},{16,24},{24,0},{1,9},{9,17},{17,25},{25,1},{2,10},{10... | collective-permute-start | bytes 1572872 | tf_op jit(solution)/shard_map/ppermute | solution.py:31
  50.2 14.8 %collective-permute-start.21 = (bf16[512,512]{1,0:T(8,128)(2,1)S(1)}, bf16[512,512]{1,0:T(8,128)(2,1)S(1)}, u32[]{:S(2)}, u32[]{:S(2)}) collective-permute-start(bf16[512,512]{1,0:T(8,128)(2,1)S(1)} %pad_maximum_fusion.1.refs_8_), channel_id=1, source_target_pairs={{0,24},{8,0},{16,8},{24,16},{1,25},{9,1},{17,9},{25,17},{2,26},{10... | collective-permute-start | bytes 1572872 | tf_op jit(solution)/shard_map/ppermute | solution.py:31
  52.7 35.4 %copy-start.1 = (bf16[544,512]{1,0:T(8,128)(2,1)}, bf16[544,512]{1,0:T(8,128)(2,1)S(1)}, u32[]{:S(2)}) copy-start(bf16[544,512]{1,0:T(8,128)(2,1)S(1)} %pad_maximum_fusion.refs_0_) | copy-start | bytes 1671172
  52.7 34.1 %copy-start.32 = (f32[16,128]{1,0:T(8,128)S(1)}, f32[16,128]{1,0:T(8,128)}, u32[]{:S(2)}) copy-start(f32[16,128]{1,0:T(8,128)} %param.20) | copy-start | bytes 24580
  53.7 16.7 %collective-permute-start.11 = (bf16[544,512]{1,0:T(8,128)(2,1)S(1)}, bf16[544,512]{1,0:T(8,128)(2,1)S(1)}, u32[]{:S(2)}, u32[]{:S(2)}) collective-permute-start(bf16[544,512]{1,0:T(8,128)(2,1)S(1)} %constant_dynamic-update-slice_fusion.refs_1_), channel_id=1, source_target_pairs={{0,32},{32,64},{64,96},{96,0},{1,33},{33,65},{65,97},{97,1},{2,34}... | collective-permute-start | bytes 1671176 | tf_op jit(solution)/shard_map/ppermute | solution.py:31
  55.3 23.7 %collective-permute-start.10 = (bf16[544,512]{1,0:T(8,128)(2,1)S(1)}, bf16[544,512]{1,0:T(8,128)(2,1)}, u32[]{:S(2)}, u32[]{:S(2)}) collective-permute-start(bf16[544,512]{1,0:T(8,128)(2,1)S(1)} %pad_maximum_fusion.refs_0_), channel_id=1, source_target_pairs={{0,32},{32,64},{64,96},{96,0},{1,33},{33,65},{65,97},{97,1},{2,34}... | collective-permute-start | bytes 1671176 | tf_op jit(solution)/shard_map/ppermute | solution.py:31
  65.1 15.1 %collective-permute-start.4 = (bf16[528,512]{1,0:T(8,128)(2,1)S(1)}, bf16[528,512]{1,0:T(8,128)(2,1)S(1)}, u32[]{:S(2)}, u32[]{:S(2)}) collective-permute-start(bf16[528,512]{1,0:T(8,128)(2,1)S(1)} %collective-permute-done.refs_1_), channel_id=1, source_target_pairs={{0,1},{1,0},{2,3},{3,2},{4,5},{5,4},{6,7},{7,6},{8,9},{9,8},{10,11... | collective-permute-start | bytes 1622024 | tf_op jit(solution)/shard_map/ppermute | solution.py:67
  65.1 16.0 %collective-permute-start.5 = (bf16[528,512]{1,0:T(8,128)(2,1)S(1)}, bf16[528,512]{1,0:T(8,128)(2,1)S(1)}, u32[]{:S(2)}, u32[]{:S(2)}) collective-permute-start(bf16[528,512]{1,0:T(8,128)(2,1)S(1)} %collective-permute-done.1.refs_2_), channel_id=1, source_target_pairs={{0,1},{1,0},{2,3},{3,2},{4,5},{5,4},{6,7},{7,6},{8,9},{9,8},{10,11... | collective-permute-start | bytes 1622024 | tf_op jit(solution)/shard_map/ppermute | solution.py:67
  65.6 17.7 %collective-permute-start.6 = (bf16[528,512]{1,0:T(8,128)(2,1)S(1)}, bf16[528,512]{1,0:T(8,128)(2,1)S(1)}, u32[]{:S(2)}, u32[]{:S(2)}) collective-permute-start(bf16[528,512]{1,0:T(8,128)(2,1)S(1)} %collective-permute-done.2.refs_3_), channel_id=1, source_target_pairs={{0,1},{1,0},{2,3},{3,2},{4,5},{5,4},{6,7},{7,6},{8,9},{9,8},{10,11... | collective-permute-start | bytes 1622024 | tf_op jit(solution)/shard_map/ppermute | solution.py:67
  70.4 23.4 %collective-permute-start.12 = (bf16[544,512]{1,0:T(8,128)(2,1)S(1)}, bf16[544,512]{1,0:T(8,128)(2,1)S(1)}, u32[]{:S(2)}, u32[]{:S(2)}) collective-permute-start(bf16[544,512]{1,0:T(8,128)(2,1)S(1)} %pad_maximum_fusion.refs_0_), channel_id=1, source_target_pairs={{0,96},{32,0},{64,32},{96,64},{1,97},{33,1},{65,33},{97,65},{2,98}... | collective-permute-start | bytes 1671176 | tf_op jit(solution)/shard_map/ppermute | solution.py:31
  79.0 16.1 %collective-permute-start.15 = (bf16[544,512]{1,0:T(8,128)(2,1)}, bf16[544,512]{1,0:T(8,128)(2,1)}, u32[]{:S(2)}, u32[]{:S(2)}) collective-permute-start(bf16[544,512]{1,0:T(8,128)(2,1)} %collective-permute-done.13.refs_5_), channel_id=1, source_target_pairs={{0,96},{32,0},{64,32},{96,64},{1,97},{33,1},{65,33},{97,65},{2,98}... | collective-permute-start | bytes 1671176 | tf_op jit(solution)/shard_map/ppermute | solution.py:31
  80.1 14.9 %collective-permute-start.14 = (bf16[544,512]{1,0:T(8,128)(2,1)}, bf16[544,512]{1,0:T(8,128)(2,1)}, u32[]{:S(2)}, u32[]{:S(2)}) collective-permute-start(bf16[544,512]{1,0:T(8,128)(2,1)} %collective-permute-done.10.refs_2_), channel_id=1, source_target_pairs={{0,32},{32,64},{64,96},{96,0},{1,33},{33,65},{65,97},{97,1},{2,34}... | collective-permute-start | bytes 1671176 | tf_op jit(solution)/shard_map/ppermute | solution.py:31
  81.1 12.8 %collective-permute-start.24 = (bf16[512,512]{1,0:T(8,128)(2,1)}, bf16[512,512]{1,0:T(8,128)(2,1)}, u32[]{:S(2)}, u32[]{:S(2)}) collective-permute-start(bf16[512,512]{1,0:T(8,128)(2,1)} %collective-permute-done.22.refs_13_), channel_id=1, source_target_pairs={{0,24},{8,0},{16,8},{24,16},{1,25},{9,1},{17,9},{25,17},{2,26},{10... | collective-permute-start | bytes 1572872 | tf_op jit(solution)/shard_map/ppermute | solution.py:31
  83.3 11.8 %collective-permute-start.23 = (bf16[512,512]{1,0:T(8,128)(2,1)}, bf16[512,512]{1,0:T(8,128)(2,1)}, u32[]{:S(2)}, u32[]{:S(2)}) collective-permute-start(bf16[512,512]{1,0:T(8,128)(2,1)} %collective-permute-done.19.refs_10_), channel_id=1, source_target_pairs={{0,8},{8,16},{16,24},{24,0},{1,9},{9,17},{17,25},{25,1},{2,10},{10... | collective-permute-start | bytes 1572872 | tf_op jit(solution)/shard_map/ppermute | solution.py:31
  103.7 34.4 %all-to-all-start = ((bf16[16,4,128,128]{3,2,1,0:T(8,128)(2,1)}), bf16[16,4,128,128]{3,2,1,0:T(8,128)(2,1)}, u32[]{:S(2)}, u32[]{:S(2)}) async-start(bf16[16,4,128,128]{3,2,1,0:T(8,128)(2,1)} %bitcast.20), calls=%async_computation | async-start | bytes 4194304 | tf_op jit(solution)/shard_map/all_to_all | solution.py:469
  109.0 5.3 %collective-permute-start.25 = (bf16[4,128,128]{2,1,0:T(8,128)(2,1)S(1)}, bf16[4,128,128]{2,1,0:T(8,128)(2,1)S(1)}, u32[]{:S(2)}, u32[]{:S(2)}) collective-permute-start(bf16[4,128,128]{2,1,0:T(8,128)(2,1)S(1)} %copy-done.46), channel_id=1, source_target_pairs={{0,1},{1,0},{2,3},{3,2},{4,5},{5,4},{6,7},{7,6},{8,9},{9,8},{10,11... | collective-permute-start | bytes 393224 | tf_op jit(solution)/shard_map/ppermute | solution.py:38
  109.1 6.6 %collective-permute-start.26 = (bf16[4,128,128]{2,1,0:T(8,128)(2,1)S(1)}, bf16[4,128,128]{2,1,0:T(8,128)(2,1)S(1)}, u32[]{:S(2)}, u32[]{:S(2)}) collective-permute-start(bf16[4,128,128]{2,1,0:T(8,128)(2,1)S(1)} %copy-done.42), channel_id=1, source_target_pairs={{0,6},{1,7},{2,0},{3,1},{4,2},{5,3},{6,4},{7,5},{8,14},{9,15},{10,... | collective-permute-start | bytes 393224 | tf_op jit(solution)/shard_map/ppermute | solution.py:38
  109.9 7.1 %collective-permute-start.27 = (bf16[4,128,128]{2,1,0:T(8,128)(2,1)S(1)}, bf16[4,128,128]{2,1,0:T(8,128)(2,1)S(1)}, u32[]{:S(2)}, u32[]{:S(2)}) collective-permute-start(bf16[4,128,128]{2,1,0:T(8,128)(2,1)S(1)} %copy-done.40), channel_id=1, source_target_pairs={{0,7},{1,6},{2,1},{3,0},{4,3},{5,2},{6,5},{7,4},{8,15},{9,14},{10,... | collective-permute-start | bytes 393224 | tf_op jit(solution)/shard_map/ppermute | solution.py:38
  110.9 7.9 %collective-permute-start.28 = (bf16[4,128,128]{2,1,0:T(8,128)(2,1)S(1)}, bf16[4,128,128]{2,1,0:T(8,128)(2,1)S(1)}, u32[]{:S(2)}, u32[]{:S(2)}) collective-permute-start(bf16[4,128,128]{2,1,0:T(8,128)(2,1)S(1)} %copy-done.39), channel_id=1, source_target_pairs={{0,4},{1,5},{2,6},{3,7},{4,0},{5,1},{6,2},{7,3},{8,12},{9,13},{10,... | collective-permute-start | bytes 393224 | tf_op jit(solution)/shard_map/ppermute | solution.py:38
  113.0 7.8 %collective-permute-start.29 = (bf16[4,128,128]{2,1,0:T(8,128)(2,1)S(1)}, bf16[4,128,128]{2,1,0:T(8,128)(2,1)S(1)}, u32[]{:S(2)}, u32[]{:S(2)}) collective-permute-start(bf16[4,128,128]{2,1,0:T(8,128)(2,1)S(1)} %copy-done.38), channel_id=1, source_target_pairs={{0,5},{1,4},{2,7},{3,6},{4,1},{5,0},{6,3},{7,2},{8,13},{9,12},{10,... | collective-permute-start | bytes 393224 | tf_op jit(solution)/shard_map/ppermute | solution.py:38
  114.3 9.7 %collective-permute-start.30 = (bf16[4,128,128]{2,1,0:T(8,128)(2,1)S(1)}, bf16[4,128,128]{2,1,0:T(8,128)(2,1)S(1)}, u32[]{:S(2)}, u32[]{:S(2)}) collective-permute-start(bf16[4,128,128]{2,1,0:T(8,128)(2,1)S(1)} %copy-done.37), channel_id=1, source_target_pairs={{0,2},{1,3},{2,4},{3,5},{4,6},{5,7},{6,0},{7,1},{8,10},{9,11},{10,... | collective-permute-start | bytes 393224 | tf_op jit(solution)/shard_map/ppermute | solution.py:38
  115.7 11.0 %collective-permute-start.31 = (bf16[4,128,128]{2,1,0:T(8,128)(2,1)S(1)}, bf16[4,128,128]{2,1,0:T(8,128)(2,1)S(1)}, u32[]{:S(2)}, u32[]{:S(2)}) collective-permute-start(bf16[4,128,128]{2,1,0:T(8,128)(2,1)S(1)} %copy-done.36), channel_id=1, source_target_pairs={{0,3},{1,2},{2,5},{3,4},{4,7},{5,6},{6,1},{7,0},{8,11},{9,10},{10,... | collective-permute-start | bytes 393224 | tf_op jit(solution)/shard_map/ppermute | solution.py:38
  149.0 40.4 %all-to-all-start.1 = ((bf16[16,4,128,128]{3,2,1,0:T(8,128)(2,1)}), bf16[16,4,128,128]{3,2,1,0:T(8,128)(2,1)}, u32[]{:S(2)}, u32[]{:S(2)}) async-start(bf16[16,4,128,128]{3,2,1,0:T(8,128)(2,1)} %bitcast.21), calls=%async_computation.1 | async-start | bytes 4194304 | tf_op jit(solution)/shard_map/all_to_all | solution.py:469
  156.3 5.8 %collective-permute-start.32 = (bf16[4,128,128]{2,1,0:T(8,128)(2,1)S(1)}, bf16[4,128,128]{2,1,0:T(8,128)(2,1)S(1)}, u32[]{:S(2)}, u32[]{:S(2)}) collective-permute-start(bf16[4,128,128]{2,1,0:T(8,128)(2,1)S(1)} %copy-done.49), channel_id=1, source_target_pairs={{0,1},{1,0},{2,3},{3,2},{4,5},{5,4},{6,7},{7,6},{8,9},{9,8},{10,11... | collective-permute-start | bytes 393224 | tf_op jit(solution)/shard_map/ppermute | solution.py:38
  156.4 6.4 %collective-permute-start.33 = (bf16[4,128,128]{2,1,0:T(8,128)(2,1)S(1)}, bf16[4,128,128]{2,1,0:T(8,128)(2,1)S(1)}, u32[]{:S(2)}, u32[]{:S(2)}) collective-permute-start(bf16[4,128,128]{2,1,0:T(8,128)(2,1)S(1)} %copy-done.48), channel_id=1, source_target_pairs={{0,6},{1,7},{2,0},{3,1},{4,2},{5,3},{6,4},{7,5},{8,14},{9,15},{10,... | collective-permute-start | bytes 393224 | tf_op jit(solution)/shard_map/ppermute | solution.py:38
  157.1 7.5 %collective-permute-start.34 = (bf16[4,128,128]{2,1,0:T(8,128)(2,1)S(1)}, bf16[4,128,128]{2,1,0:T(8,128)(2,1)S(1)}, u32[]{:S(2)}, u32[]{:S(2)}) collective-permute-start(bf16[4,128,128]{2,1,0:T(8,128)(2,1)S(1)} %copy-done.47), channel_id=1, source_target_pairs={{0,7},{1,6},{2,1},{3,0},{4,3},{5,2},{6,5},{7,4},{8,15},{9,14},{10,... | collective-permute-start | bytes 393224 | tf_op jit(solution)/shard_map/ppermute | solution.py:38
  159.0 7.9 %collective-permute-start.35 = (bf16[4,128,128]{2,1,0:T(8,128)(2,1)S(1)}, bf16[4,128,128]{2,1,0:T(8,128)(2,1)S(1)}, u32[]{:S(2)}, u32[]{:S(2)}) collective-permute-start(bf16[4,128,128]{2,1,0:T(8,128)(2,1)S(1)} %copy-done.45), channel_id=1, source_target_pairs={{0,4},{1,5},{2,6},{3,7},{4,0},{5,1},{6,2},{7,3},{8,12},{9,13},{10,... | collective-permute-start | bytes 393224 | tf_op jit(solution)/shard_map/ppermute | solution.py:38
  160.4 8.2 %collective-permute-start.36 = (bf16[4,128,128]{2,1,0:T(8,128)(2,1)S(1)}, bf16[4,128,128]{2,1,0:T(8,128)(2,1)S(1)}, u32[]{:S(2)}, u32[]{:S(2)}) collective-permute-start(bf16[4,128,128]{2,1,0:T(8,128)(2,1)S(1)} %copy-done.44), channel_id=1, source_target_pairs={{0,5},{1,4},{2,7},{3,6},{4,1},{5,0},{6,3},{7,2},{8,13},{9,12},{10,... | collective-permute-start | bytes 393224 | tf_op jit(solution)/shard_map/ppermute | solution.py:38
  162.2 9.7 %collective-permute-start.37 = (bf16[4,128,128]{2,1,0:T(8,128)(2,1)S(1)}, bf16[4,128,128]{2,1,0:T(8,128)(2,1)S(1)}, u32[]{:S(2)}, u32[]{:S(2)}) collective-permute-start(bf16[4,128,128]{2,1,0:T(8,128)(2,1)S(1)} %copy-done.43), channel_id=1, source_target_pairs={{0,2},{1,3},{2,4},{3,5},{4,6},{5,7},{6,0},{7,1},{8,10},{9,11},{10,... | collective-permute-start | bytes 393224 | tf_op jit(solution)/shard_map/ppermute | solution.py:38
  162.9 11.7 %collective-permute-start.38 = (bf16[4,128,128]{2,1,0:T(8,128)(2,1)S(1)}, bf16[4,128,128]{2,1,0:T(8,128)(2,1)S(1)}, u32[]{:S(2)}, u32[]{:S(2)}) collective-permute-start(bf16[4,128,128]{2,1,0:T(8,128)(2,1)S(1)} %copy-done.41), channel_id=1, source_target_pairs={{0,3},{1,2},{2,5},{3,4},{4,7},{5,6},{6,1},{7,0},{8,11},{9,10},{10,... | collective-permute-start | bytes 393224 | tf_op jit(solution)/shard_map/ppermute | solution.py:38
  (43 other events, 437.0 us)
